TPU v7x, 32 devices: a whole 2x2x4 slice. The times are simulated.
32 devices in a mesh: rows: 32 (over z, y, x, core).
Axes of the slice: x: 2, y: 2, z: 4, core: 2. Of those that a mesh axis runs over, the one named last changes fastest.
Arguments:
- snapshots: float32 [16384, 512], P('rows'), may hold values from -100 to 100
- validation: float32 [16384, 512], P('rows'), may hold values from -100 to 100
- eigenvectors: float32 [512, 64], replicated, may hold values from -0.25 to 0.25
- eigenvalues: float32 [64], replicated, may hold values from 16 to 256
Outputs:
- gram: float32 [512, 512], replicated
- modes: float32 [64, 16384], P(None, 'rows')
- train_coef: float32 [64, 512], replicated
- valid_coef: float32 [64, 512], replicated
All inputs are finite; a program needn't handle non-finite values.
Results may differ from a plain program's by a relative error of at most 0.000071.
Values sent between devices are 32-bit elements; how exact they have to be, the bound alone decides.
No kernel may reach another device: no remote copies, remote signals or barrier semaphores. Data moves between devices by JAX's collectives and lax.ppermute only.
A program may use at most 64 MiB of HBM per device.

v0:
```python
import jax
import jax.numpy as jnp
from jax import lax
from jax.sharding import PartitionSpec as P


def body(snapshots, validation, eigenvectors, eigenvalues):
    highest = lax.Precision.HIGHEST
    devices = lax.axis_size("rows")
    total = snapshots.shape[0] * devices * 1.0
    gram_part = (
        lax.dot_general(
            snapshots,
            snapshots,
            (((0,), (0,)), ((), ())),
            precision=highest,
            preferred_element_type=jnp.float32,
        )
        / total
    )
    scales = lax.rsqrt(eigenvalues)
    modes = (
        lax.dot_general(
            eigenvectors,
            snapshots,
            (((0,), (1,)), ((), ())),
            precision=highest,
            preferred_element_type=jnp.float32,
        )
        * scales[:, None]
    )
    gram = lax.psum(gram_part, "rows")
    valid_part = (
        jnp.dot(modes, validation, precision=highest, preferred_element_type=jnp.float32) / total
    )
    valid_coef = lax.psum(valid_part, "rows")
    train_coef = (
        lax.dot_general(
            eigenvectors,
            gram,
            (((0,), (0,)), ((), ())),
            precision=highest,
            preferred_element_type=jnp.float32,
        )
        * scales[:, None]
    )
    return (gram, modes, train_coef, valid_coef)


def solution(mesh):
    in_specs = (P("rows", None), P("rows", None), P(), P())
    out_specs = (P(), P(None, "rows"), P(), P())
    return jax.shard_map(body, mesh=mesh, in_specs=in_specs, out_specs=out_specs, check_vma=False)
```

profile of v0, /device:TPU:0, one launch (start us, length us, event | category | flops | bytes accessed | tf_op | source)
XLA Modules:
  0.0 159.9 jit_solution(1666710015621987377)
XLA Ops:
  7.2 0.0 copy-start
  7.2 0.0 all-reduce.3.cloned.1.call-start
  7.2 0.7 rsqrt.3
  8.0 0.4 copy-done
  8.4 0.0 copy-start.3
  8.4 2.8 %convolution_multiply_fusion = f32[512,512]{1,0:T(8,128)} fusion(f32[512,512]{1,0:T(8,128)S(1)} %copy-done), kind=kOutput, calls=%fused_computation | convolution fusion | flops 1610874880 | bytes 2097152 | tf_op jit(solution)/shard_map/dot_general | solution.py:12
  11.2 0.0 copy-done.3
  11.2 0.0 copy-start.2
  11.2 1.1 convolution_multiply_fusion.3
  12.4 0.1 copy-done.2
  12.5 0.0 copy-start.4
  12.5 1.4 convolution_multiply_fusion.1
  13.9 0.0 copy-done.4
  13.9 0.0 all-reduce.3.cloned.1.call-update
  13.9 134.7 %all-reduce.3.cloned.1.call-done = (f32[512,512]{1,0:T(8,128)}, f32[64,512]{1,0:T(8,128)}) async-done(((f32[512,512]{1,0:T(8,128)}, f32[64,512]{1,0:T(8,128)}), (f32[512,512]{1,0:T(8,128)}, f32[64,512]{1,0:T(8,128)})) %all-reduce.3.cloned.1.call-update) | async-done | bytes 1179664 | tf_op jit(solution)/shard_map/psum | solution.py:32
  148.7 0.0 copy-start.1
  148.7 2.8 %fusion = f32[64,512]{1,0:T(8,128)} fusion(f32[512,512]{1,0:T(8,128)} %get-tuple-element.6, f32[512,64]{0,1:T(8,128)S(1)} %copy-done.3, f32[64]{0:T(128)S(1)} %rsqrt.3), kind=kOutput, calls=%fused_computation.3 | convolution fusion | flops 201359360 | bytes 1310976 | tf_op jit(solution)/shard_map/dot_general | solution.py:38
  151.4 0.0 copy-done.1
  151.4 0.0 copy-start.5
  151.4 1.0 copy.10
  152.4 0.1 copy-done.5
  152.4 0.7 copy.11
Async XLA Ops:
  7.2 1.2 copy-start
  7.2 141.5 %all-reduce.3.cloned.1.call-start = ((), (), s32[]{:S(2)}) async-start(), calls=%async_computation | async-start | bytes 2359296 | tf_op jit(solution)/shard_map/psum | solution.py:32
  8.4 2.8 %copy-start.3 = (f32[512,64]{0,1:T(8,128)S(1)}, f32[512,64]{0,1:T(8,128)}, u32[]{:S(2)}) copy-start(f32[512,64]{0,1:T(8,128)} %param.6) | copy-start | bytes 393220
  11.2 1.2 copy-start.2
  12.5 1.4 copy-start.4
  148.7 2.8 %copy-start.1 = (f32[512,512]{1,0:T(8,128)S(1)}, f32[512,512]{1,0:T(8,128)}, u32[]{:S(2)}) copy-start(f32[512,512]{1,0:T(8,128)} %get-tuple-element.6) | copy-start | bytes 3145732
  151.4 1.0 copy-start.5
Sparse Core Ops, SparseCore 0:
  14.0 134.5 all-reduce.2
where the time goes:
time: 160 us
  waiting for transfers between devices  135 us (84%)
  between operations  14 us (9%)
  matrix products  8.12 us (5%)
  local copies, waits for them, and re-layouts  2.99 us (2%)
    psum x1, waiting for transfers between devices, body(): gram = lax.psum(gram_part, 'rows')  135 us
  transfers between devices with their start and end apart: 1, of which 1 were waited for; matrix products, arithmetic and copies ran while one was open for 0% of the time, Pallas kernels for 0%

commit v1 on v0

v1 whole, which is shorter than its diff:
```python
import jax
import jax.numpy as jnp
from jax import lax
from jax.sharding import Mesh, PartitionSpec as P

BLOCK = 128
DIRECT = 4


def axes_of(mesh):
    devices = list(mesh.devices.flat)
    cores = len({d.core_on_chip for d in devices})
    planes = len({d.coords[2] for d in devices})
    chips = len(devices) // (cores * planes)
    return Mesh(mesh.devices.reshape(planes, chips, cores), ("plane", "chip", "core"))


def partners(n, r):
    return [(i, i ^ r) for i in range(n)]


def tree(parts):
    while len(parts) > 1:
        parts = [a + b for a, b in zip(parts[::2], parts[1::2], strict=True)]
    return parts[0]


def direct(n):
    return n <= DIRECT and n & (n - 1) == 0


def reduce_scatter(x, axis):
    n = lax.axis_size(axis)
    if not direct(n):
        return lax.psum_scatter(x, axis)
    me = lax.axis_index(axis)
    parts = [lax.dynamic_index_in_dim(x, me ^ r, 0, False) for r in range(n)]
    return tree([p if r == 0 else lax.ppermute(p, axis, partners(n, r)) for r, p in enumerate(parts)])


def all_reduce(x, axis):
    n = lax.axis_size(axis)
    if not direct(n):
        return lax.psum(x, axis)
    return tree([x if r == 0 else lax.ppermute(x, axis, partners(n, r)) for r in range(n)])


def body(snapshots, validation, eigenvectors, eigenvalues):
    high = lax.Precision.HIGH
    cores, chips = lax.axis_size("core"), lax.axis_size("chip")
    devices = cores * chips * lax.axis_size("plane")
    total = snapshots.shape[0] * devices * 1.0
    k, m = eigenvectors.shape
    blocks = k // BLOCK
    dot = lambda a, b, dims, p: lax.dot_general(a, b, (dims, ((), ())), precision=p, preferred_element_type=jnp.float32)
    scales = lax.rsqrt(eigenvalues)
    gram_part = dot(snapshots, snapshots, ((0,), (0,)), high) / total
    modes = dot(eigenvectors, snapshots, ((0,), (1,)), high) * scales[:, None]
    valid_part = dot(modes, validation, ((1,), (0,)), high) / total

    upper = [(i, j) for i in range(blocks) for j in range(i, blocks)]
    cut = lambda a, i, j: a[i * BLOCK : (i + 1) * BLOCK, j * BLOCK : (j + 1) * BLOCK]
    packed = jnp.concatenate([cut(gram_part, i, j) for i, j in upper] + [valid_part[:, j * BLOCK : (j + 1) * BLOCK] for j in range(blocks)], 0)
    rows = packed.shape[0]
    piece = -(-rows // (cores * chips * 8)) * 8
    packed = jnp.pad(packed, ((0, cores * chips * piece - rows), (0, 0)))

    own = reduce_scatter(packed.reshape(chips, cores, piece, BLOCK).swapaxes(0, 1), "core")
    own = reduce_scatter(own, "chip")
    own = all_reduce(own, "plane")
    packed = lax.all_gather(own, ("chip", "core"), tiled=True)

    at = {ij: packed[n * BLOCK : (n + 1) * BLOCK] for n, ij in enumerate(upper)}
    gram = jnp.concatenate(
        [jnp.concatenate([at[i, j] if i <= j else at[j, i].T for j in range(blocks)], 1) for i in range(blocks)], 0
    )
    base = len(upper) * BLOCK
    valid_coef = jnp.concatenate([packed[base + j * m : base + (j + 1) * m] for j in range(blocks)], 1)
    train_coef = dot(eigenvectors, gram, ((0,), (0,)), high) * scales[:, None]
    return gram, modes, train_coef, valid_coef


def solution(mesh):
    inner = axes_of(mesh)
    rows = ("plane", "chip", "core")
    in_specs = (P(rows, None), P(rows, None), P(), P())
    out_specs = (P(), P(None, rows), P(), P())
    return jax.shard_map(body, mesh=inner, in_specs=in_specs, out_specs=out_specs, check_vma=False)
```

time: 160 us -> 41.5 us (0.26)
  waiting for transfers between devices: 135 us -> 13.1 us
  between operations: 14 us -> 0.91 us
  blocking collectives: 0 us -> 10.6 us
  starting transfers between devices: 0.04 us -> 9.46 us
  matrix products: 8.12 us -> 3.19 us
    psum x1 -> x0, waiting for transfers between devices: 135 us -> none  [body(): gram = lax.psum(gram_part, 'rows')]
    ppermute x0 -> x7, waiting for transfers between devices: none -> 13.1 us  [the longest x4 6.84 us: reduce_scatter(): lax.ppermute(p, axis, partners(n, r))]
    all_gather x0 -> x1, blocking collectives: none -> 10.6 us  [body(): packed = lax.all_gather(own, ('chip', 'core'), tiled=True)]
    ppermute x0 -> x7, starting transfers between devices: none -> 9.46 us  [the longest x4 5.01 us: reduce_scatter(): lax.ppermute(p, axis, partners(n, r))]
    dot_general x4, matrix products: 8.12 us -> 3.19 us  [body(): lax.dot_general(a, b, (dims, ((), ())), precision=p, preferred_element_ty...]
  transfers between devices with their start and end apart: 1 -> 7, of which waited for: 1 -> 7; matrix products, arithmetic and copies ran while one was open for 0% -> 0% of each run, Pallas kernels for 0% -> 0%
where the time goes in v1:
time: 41.5 us; the launch traced here: 41.3 us
  waiting for transfers between devices  13.1 us (32%)
  blocking collectives  10.6 us (26%)
  starting transfers between devices  9.46 us (23%)
  matrix products  3.19 us (8%)
  local copies, waits for them, and re-layouts  3.16 us (8%)
  between operations  0.91 us (2%)
  other arithmetic  0.85 us (2%)
    all_gather x1, blocking collectives, body(): packed = lax.all_gather(own, ('chip', 'core'), tiled=True)  10.6 us
    ppermute x4, waiting for transfers between devices, reduce_scatter(): lax.ppermute(p, axis, partners(n, r))  6.84 us
    ppermute x3, waiting for transfers between devices, all_reduce(): lax.ppermute(x, axis, partners(n, r))  6.29 us
    ppermute x4, starting transfers between devices, reduce_scatter(): lax.ppermute(p, axis, partners(n, r))  5.01 us
    ppermute x3, starting transfers between devices, all_reduce(): lax.ppermute(x, axis, partners(n, r))  4.45 us
    dot_general x4, matrix products, body(): lax.dot_general(a, b, (dims, ((), ())), precision=p, preferred_element_ty...  3.19 us
    unnamed x27, local copies, waits for them, and re-layouts  2.59 us
  transfers between devices with their start and end apart: 7, of which 7 were waited for; matrix products, arithmetic and copies ran while one was open for 0% of the time, Pallas kernels for 0%

profile of v1, /device:TPU:0, one launch (start us, length us, event | category | flops | bytes accessed | tf_op | source)
XLA Modules:
  0.0 41.3 jit_solution(2584023325631515082)
XLA Ops:
  0.6 1.2 %copy-done = f32[512,512]{1,0:T(8,128)S(1)} copy-done((f32[512,512]{1,0:T(8,128)S(1)}, f32[512,512]{1,0:T(8,128)}, u32[]{:S(2)}) %copy-start) | copy-done | bytes 1048600
  1.9 1.0 %convolution_multiply_fusion = f32[512,512]{1,0:T(8,128)S(1)} fusion(f32[512,512]{1,0:T(8,128)S(1)} %copy-done), kind=kOutput, calls=%fused_computation | convolution fusion | flops 805568512 | bytes 2097152 | tf_op jit(solution)/shard_map/dot_general | solution.py:55
  3.1 0.5 %copy-done.5 = f32[64]{0:T(128)S(1)} copy-done((f32[64]{0:T(128)S(1)}, f32[64]{0:T(128)}, u32[]{:S(2)}) %copy-start.5) | copy-done | bytes 280
  3.6 0.3 copy-done.3
  3.9 0.6 %convolution_multiply_fusion.3 = f32[64,512]{1,0:T(8,128)S(1)} fusion(f32[512,64]{0,1:T(8,128)S(1)} %copy-done.3, f32[512,512]{1,0:T(8,128)S(1)} %copy-done, f32[64]{0:T(128)S(1)} %rsqrt.3), kind=kOutput, calls=%fused_computation.4 | convolution fusion | flops 100696064 | bytes 1310976 | tf_op jit(solution)/shard_map/dot_general | solution.py:55
  4.5 0.5 %convolution_multiply_fusion.2 = f32[64,512]{1,0:T(8,128)S(1)} fusion(f32[64,512]{1,0:T(8,128)S(1)} %convolution_multiply_fusion.3, f32[512,512]{1,0:T(8,128)S(1)} %copy-done.2), kind=kOutput, calls=%fused_computation.3 | convolution fusion | flops 100696064 | bytes 1310720 | tf_op jit(solution)/shard_map/dot_general | solution.py:55
  5.0 0.2 copy-done.4
  5.2 0.6 %collective-permute-start = (f32[4,192,128]{2,1,0:T(8,128)S(1)}, f32[4,192,128]{2,1,0:T(8,128)S(1)}, u32[]{:S(2)}, u32[]{:S(2)}) collective-permute-start(f32[4,192,128]{2,1,0:T(8,128)S(1)} %dynamic-slice_bitcast_fusion), channel_id=1, source_target_pairs={{0,1},{1,0},{2,3},{3,2},{4,5},{5,4},{6,7},{7,6},{8,9},{9,8},{10,11... | collective-permute-start | bytes 1179656 | tf_op jit(solution)/shard_map/ppermute | solution.py:38
  5.8 1.3 %collective-permute-done = f32[4,192,128]{2,1,0:T(8,128)S(1)} collective-permute-done((f32[4,192,128]{2,1,0:T(8,128)S(1)}, f32[4,192,128]{2,1,0:T(8,128)S(1)}, u32[]{:S(2)}, u32[]{:S(2)}) %collective-permute-start) | collective-permute-done | bytes 393248 | tf_op jit(solution)/shard_map/ppermute | solution.py:38
  7.2 2.9 %collective-permute-start.1 = (f32[192,128]{1,0:T(8,128)S(1)}, f32[192,128]{1,0:T(8,128)S(1)}, u32[]{:S(2)}, u32[]{:S(2)}) collective-permute-start(f32[192,128]{1,0:T(8,128)S(1)} %get-tuple-element.24), channel_id=1, source_target_pairs={{0,2},{2,0},{4,6},{6,4},{1,3},{3,1},{5,7},{7,5},{8,10},{10,8},{12,... | collective-permute-start | bytes 294920 | tf_op jit(solution)/shard_map/ppermute | solution.py:38
  10.2 1.5 %collective-permute-start.2 = (f32[192,128]{1,0:T(8,128)S(1)}, f32[192,128]{1,0:T(8,128)S(1)}, u32[]{:S(2)}, u32[]{:S(2)}) collective-permute-start(f32[192,128]{1,0:T(8,128)S(1)} %get-tuple-element.23), channel_id=1, source_target_pairs={{0,4},{2,6},{4,0},{6,2},{1,5},{3,7},{5,1},{7,3},{8,12},{10,14},{12... | collective-permute-start | bytes 294920 | tf_op jit(solution)/shard_map/ppermute | solution.py:38
  11.7 1.6 %collective-permute-done.1 = f32[192,128]{1,0:T(8,128)S(1)} collective-permute-done((f32[192,128]{1,0:T(8,128)S(1)}, f32[192,128]{1,0:T(8,128)S(1)}, u32[]{:S(2)}, u32[]{:S(2)}) %collective-permute-start.1) | collective-permute-done | bytes 98336 | tf_op jit(solution)/shard_map/ppermute | solution.py:38
  13.3 2.6 %collective-permute-done.2 = f32[192,128]{1,0:T(8,128)S(1)} collective-permute-done((f32[192,128]{1,0:T(8,128)S(1)}, f32[192,128]{1,0:T(8,128)S(1)}, u32[]{:S(2)}, u32[]{:S(2)}) %collective-permute-start.2) | collective-permute-done | bytes 98336 | tf_op jit(solution)/shard_map/ppermute | solution.py:38
  15.9 1.3 %collective-permute-done.3 = f32[192,128]{1,0:T(8,128)S(1)} collective-permute-done((f32[192,128]{1,0:T(8,128)S(1)}, f32[192,128]{1,0:T(8,128)S(1)}, u32[]{:S(2)}, u32[]{:S(2)}) %collective-permute-start.3) | collective-permute-done | bytes 98336 | tf_op jit(solution)/shard_map/ppermute | solution.py:38
  17.2 1.6 %collective-permute-start.4 = (f32[192,128]{1,0:T(8,128)S(1)}, f32[192,128]{1,0:T(8,128)S(1)}, u32[]{:S(2)}, u32[]{:S(2)}) collective-permute-start(f32[192,128]{1,0:T(8,128)S(1)} %fusion.1), channel_id=1, source_target_pairs={{0,8},{8,0},{16,24},{24,16},{1,9},{9,1},{17,25},{25,17},{2,10},{10... | collective-permute-start | bytes 294920 | tf_op jit(solution)/shard_map/ppermute | solution.py:45
  18.9 2.6 %collective-permute-start.5 = (f32[192,128]{1,0:T(8,128)S(1)}, f32[192,128]{1,0:T(8,128)S(1)}, u32[]{:S(2)}, u32[]{:S(2)}) collective-permute-start(f32[192,128]{1,0:T(8,128)S(1)} %fusion.1), channel_id=1, source_target_pairs={{0,16},{8,24},{16,0},{24,8},{1,17},{9,25},{17,1},{25,9},{2,18},{10... | collective-permute-start | bytes 294920 | tf_op jit(solution)/shard_map/ppermute | solution.py:45
  21.4 0.2 collective-permute-start.6
  21.7 0.9 %collective-permute-done.4 = f32[192,128]{1,0:T(8,128)S(1)} collective-permute-done((f32[192,128]{1,0:T(8,128)S(1)}, f32[192,128]{1,0:T(8,128)S(1)}, u32[]{:S(2)}, u32[]{:S(2)}) %collective-permute-start.4) | collective-permute-done | bytes 98336 | tf_op jit(solution)/shard_map/ppermute | solution.py:45
  22.6 4.3 %collective-permute-done.5 = f32[192,128]{1,0:T(8,128)S(1)} collective-permute-done((f32[192,128]{1,0:T(8,128)S(1)}, f32[192,128]{1,0:T(8,128)S(1)}, u32[]{:S(2)}, u32[]{:S(2)}) %collective-permute-start.5) | collective-permute-done | bytes 98336 | tf_op jit(solution)/shard_map/ppermute | solution.py:45
  26.9 1.1 %collective-permute-done.6 = f32[192,128]{1,0:T(8,128)S(1)} collective-permute-done((f32[192,128]{1,0:T(8,128)S(1)}, f32[192,128]{1,0:T(8,128)S(1)}, u32[]{:S(2)}, u32[]{:S(2)}) %collective-permute-start.6) | collective-permute-done | bytes 98336 | tf_op jit(solution)/shard_map/ppermute | solution.py:45
  28.0 10.6 %all_gather.3 = f32[1536,128]{1,0:T(8,128)S(1)} all-gather(f32[192,128]{1,0:T(8,128)S(1)} %add_add_fusion), channel_id=1, replica_groups=mesh['plane'=4,'chip'=4,'core'=2] {'chip','core'}, dimensions={0}, use_global_device_ids=true | all-gather | bytes 884736 | tf_op jit(solution)/shard_map/all_gather | solution.py:71
  38.6 0.1 fusion.3
  38.7 0.1 copy.15
  38.8 0.1 copy.16
  38.9 0.1 copy.17
  39.0 0.1 copy.14
  39.2 0.1 copy.11
  39.3 0.1 copy.12
  39.4 0.1 copy.13
  39.5 0.1 maximum_maximum_fusion
  39.6 1.1 %fusion = f32[64,512]{1,0:T(8,128)} fusion(f32[512,512]{1,0:T(8,128)S(1)} %maximum_maximum_fusion, f32[512,64]{0,1:T(8,128)S(1)} %copy-done.3, f32[64]{0:T(128)S(1)} %rsqrt.3), kind=kOutput, calls=%fused_computation.2 | convolution fusion | flops 100696064 | bytes 1310976 | tf_op jit(solution)/shard_map/dot_general | solution.py:55
  40.7 0.7 %pad_maximum_fusion.1 = f32[64,512]{1,0:T(8,128)} fusion(f32[64,128]{1,0:T(8,128)S(1)} %get-tuple-element.7, f32[64,128]{1,0:T(8,128)S(1)} %get-tuple-element.6, f32[64,128]{1,0:T(8,128)S(1)} %get-tuple-element.5, f32[64,128]{1,0:T(8,128)S(1)} %get-tuple-element.4), kind=kLoop, calls=%fused_computation.10 | loop fusion | flops 98304 | bytes 262144 | tf_op jit(solution)/shard_map/concatenate | solution.py:78
  (30 shorter events, 0.4 us)
Async XLA Ops:
  0.6 1.2 %copy-start = (f32[512,512]{1,0:T(8,128)S(1)}, f32[512,512]{1,0:T(8,128)}, u32[]{:S(2)}) copy-start(f32[512,512]{1,0:T(8,128)} %param.4) | copy-start | bytes 3145732
  3.0 0.7 %copy-start.5 = (f32[64]{0:T(128)S(1)}, f32[64]{0:T(128)}, u32[]{:S(2)}) copy-start(f32[64]{0:T(128)} %param.7) | copy-start | bytes 772
  3.0 0.9 %copy-start.3 = (f32[512,64]{0,1:T(8,128)S(1)}, f32[512,64]{0,1:T(8,128)}, u32[]{:S(2)}) copy-start(f32[512,64]{0,1:T(8,128)} %param.6) | copy-start | bytes 393220
  3.0 1.5 %copy-start.2 = (f32[512,512]{1,0:T(8,128)S(1)}, f32[512,512]{1,0:T(8,128)}, u32[]{:S(2)}) copy-start(f32[512,512]{1,0:T(8,128)} %param.5) | copy-start | bytes 3145732
  4.5 0.7 %copy-start.4 = (f32[64,512]{1,0:T(8,128)}, f32[64,512]{1,0:T(8,128)S(1)}, u32[]{:S(2)}) copy-start(f32[64,512]{1,0:T(8,128)S(1)} %convolution_multiply_fusion.3) | copy-start | bytes 393220
  5.2 1.9 %collective-permute-start = (f32[4,192,128]{2,1,0:T(8,128)S(1)}, f32[4,192,128]{2,1,0:T(8,128)S(1)}, u32[]{:S(2)}, u32[]{:S(2)}) collective-permute-start(f32[4,192,128]{2,1,0:T(8,128)S(1)} %dynamic-slice_bitcast_fusion), channel_id=1, source_target_pairs={{0,1},{1,0},{2,3},{3,2},{4,5},{5,4},{6,7},{7,6},{8,9},{9,8},{10,11... | collective-permute-start | bytes 1179656 | tf_op jit(solution)/shard_map/ppermute | solution.py:38
  7.2 6.1 %collective-permute-start.1 = (f32[192,128]{1,0:T(8,128)S(1)}, f32[192,128]{1,0:T(8,128)S(1)}, u32[]{:S(2)}, u32[]{:S(2)}) collective-permute-start(f32[192,128]{1,0:T(8,128)S(1)} %get-tuple-element.24), channel_id=1, source_target_pairs={{0,2},{2,0},{4,6},{6,4},{1,3},{3,1},{5,7},{7,5},{8,10},{10,8},{12,... | collective-permute-start | bytes 294920 | tf_op jit(solution)/shard_map/ppermute | solution.py:38
  10.2 5.8 %collective-permute-start.2 = (f32[192,128]{1,0:T(8,128)S(1)}, f32[192,128]{1,0:T(8,128)S(1)}, u32[]{:S(2)}, u32[]{:S(2)}) collective-permute-start(f32[192,128]{1,0:T(8,128)S(1)} %get-tuple-element.23), channel_id=1, source_target_pairs={{0,4},{2,6},{4,0},{6,2},{1,5},{3,7},{5,1},{7,3},{8,12},{10,14},{12... | collective-permute-start | bytes 294920 | tf_op jit(solution)/shard_map/ppermute | solution.py:38
  11.7 5.5 %collective-permute-start.3 = (f32[192,128]{1,0:T(8,128)S(1)}, f32[192,128]{1,0:T(8,128)S(1)}, u32[]{:S(2)}, u32[]{:S(2)}) collective-permute-start(f32[192,128]{1,0:T(8,128)S(1)} %get-tuple-element.22), channel_id=1, source_target_pairs={{0,6},{2,4},{4,2},{6,0},{1,7},{3,5},{5,3},{7,1},{8,14},{10,12},{12... | collective-permute-start | bytes 294920 | tf_op jit(solution)/shard_map/ppermute | solution.py:38
  17.2 5.3 %collective-permute-start.4 = (f32[192,128]{1,0:T(8,128)S(1)}, f32[192,128]{1,0:T(8,128)S(1)}, u32[]{:S(2)}, u32[]{:S(2)}) collective-permute-start(f32[192,128]{1,0:T(8,128)S(1)} %fusion.1), channel_id=1, source_target_pairs={{0,8},{8,0},{16,24},{24,16},{1,9},{9,1},{17,25},{25,17},{2,10},{10... | collective-permute-start | bytes 294920 | tf_op jit(solution)/shard_map/ppermute | solution.py:45
  18.9 8.0 %collective-permute-start.5 = (f32[192,128]{1,0:T(8,128)S(1)}, f32[192,128]{1,0:T(8,128)S(1)}, u32[]{:S(2)}, u32[]{:S(2)}) collective-permute-start(f32[192,128]{1,0:T(8,128)S(1)} %fusion.1), channel_id=1, source_target_pairs={{0,16},{8,24},{16,0},{24,8},{1,17},{9,25},{17,1},{25,9},{2,18},{10... | collective-permute-start | bytes 294920 | tf_op jit(solution)/shard_map/ppermute | solution.py:45
  21.4 6.5 %collective-permute-start.6 = (f32[192,128]{1,0:T(8,128)S(1)}, f32[192,128]{1,0:T(8,128)S(1)}, u32[]{:S(2)}, u32[]{:S(2)}) collective-permute-start(f32[192,128]{1,0:T(8,128)S(1)} %fusion.1), channel_id=1, source_target_pairs={{0,24},{8,16},{16,8},{24,0},{1,25},{9,17},{17,9},{25,1},{2,26},{10... | collective-permute-start | bytes 294920 | tf_op jit(solution)/shard_map/ppermute | solution.py:45
  39.6 1.8 %copy-start.1 = (f32[512,512]{1,0:T(8,128)}, f32[512,512]{1,0:T(8,128)S(1)}, u32[]{:S(2)}) copy-start(f32[512,512]{1,0:T(8,128)S(1)} %maximum_maximum_fusion) | copy-start | bytes 3145732

commit v2 on v1

v2 whole, which is shorter than its diff:
```python
import functools

import jax
import jax.numpy as jnp
from jax import lax
from jax.experimental import pallas as pl
from jax.experimental.pallas import tpu as pltpu
from jax.sharding import Mesh, PartitionSpec as P

LANES = 128
DIRECT = 4
F32 = jnp.float32


def axes_of(mesh):
    devices = list(mesh.devices.flat)
    cores = len({d.core_on_chip for d in devices})
    planes = len({d.coords[2] for d in devices})
    chips = len(devices) // (cores * planes)
    return Mesh(mesh.devices.reshape(planes, chips, cores), ("plane", "chip", "core"))


def layout(k, m):
    half = k // 2
    square = half * half // LANES
    mixed, cross, valid = 0, square, 2 * square
    diagonal = valid + m * k // LANES
    return mixed, cross, valid, diagonal, diagonal + half // LANES


def split(x):
    high = x.astype(jnp.bfloat16)
    return high, (x - high.astype(F32)).astype(jnp.bfloat16)


def dot(a, b, ca, cb):
    return lax.dot_general(a, b, (((ca,), (cb,)), ((), ())), preferred_element_type=F32)


def column(row, m):
    r, c = (lax.broadcasted_iota(jnp.int32, (m, m), d) for d in (0, 1))
    return jnp.sum(jnp.where(r == c, jnp.broadcast_to(row, (m, m)), 0.0), axis=1, keepdims=True)


def order(half):
    r, c = (lax.broadcasted_iota(jnp.int32, (half, half), d) for d in (0, 1))
    return r, c


def head_kernel(
    total, s_hbm, v_hbm, e_hbm, w_hbm, packed_ref, modes_hbm, e_out, scale_out, s_buf, v_buf, e_buf, w_buf, modes_ref, sems
):
    n, k = s_buf.shape
    m = e_buf.shape[0]
    half, step = k // 2, n // 2
    mixed, cross, valid, diagonal, rows = layout(k, m)
    copies = []
    halves = [pl.ds(i * step, step) for i in range(2)]
    for src, buf in [
        *((s_hbm.at[at], s_buf.at[at]) for at in halves), (e_hbm, e_buf), (w_hbm, w_buf),
        *((v_hbm.at[at], v_buf.at[at]) for at in halves),
    ]:
        copies.append(pltpu.make_async_copy(src, buf, sems.at[len(copies)]))
        copies[-1].start()
    a = b = c = None
    modes = []
    for i in range(2):
        copies[i].wait()
        high, low = split(s_buf[i * step : (i + 1) * step, :])
        ha, hb, la, lb = high[:, :half], high[:, half:], low[:, :half], low[:, half:]
        da = dot(ha, ha, 0, 0) + dot(ha, la, 0, 0) + dot(la, ha, 0, 0)
        db = dot(ha, hb, 0, 0) + dot(ha, lb, 0, 0) + dot(la, hb, 0, 0)
        dc = dot(hb, hb, 0, 0) + dot(hb, lb, 0, 0) + dot(lb, hb, 0, 0)
        a, b, c = (da, db, dc) if i == 0 else (a + da, b + db, c + dc)
        if i == 0:
            copies[2].wait()
            copies[3].wait()
            scales = column(lax.rsqrt(w_buf[...]), m)
            e_high, e_low = split(e_buf[...])
            e_both = jnp.concatenate([e_high, e_low], 0)
            e_out[...] = e_both
            scale_out[...] = jnp.broadcast_to(scales, scale_out.shape)
        both = dot(e_both, high, 1, 1)
        modes.append((both[:m] + both[m:] + dot(e_high, low, 1, 1)) * scales)
        modes_ref[:, i * step : (i + 1) * step] = modes[i]
    modes_out = pltpu.make_async_copy(modes_ref, modes_hbm, sems.at[6])
    modes_out.start()
    r, col = order(half)
    square = jnp.where(col >= r, a, c) * (1.0 / total)
    b = b * (1.0 / total)
    last = jnp.sum(jnp.where(col == r, c, 0.0), axis=0, keepdims=True) * (1.0 / total)
    for j in range(half // LANES):
        lanes = slice(j * LANES, (j + 1) * LANES)
        packed_ref[mixed + j * half : mixed + (j + 1) * half, :] = square[:, lanes]
        packed_ref[cross + j * half : cross + (j + 1) * half, :] = b[:, lanes]
    pad = packed_ref.shape[0] - diagonal
    packed_ref[diagonal:, :] = jnp.concatenate(
        [last[:, j * LANES : (j + 1) * LANES] for j in range(half // LANES)]
        + [jnp.zeros((pad - half // LANES, LANES), F32)], 0
    )
    out = None
    for i in range(2):
        copies[4 + i].wait()
        m_high, m_low = split(modes[i])
        v_high, v_low = split(v_buf[i * step : (i + 1) * step, :])
        both = dot(jnp.concatenate([m_high, m_low], 0), v_high, 1, 0)
        part = both[:m] + both[m:] + dot(m_high, v_low, 1, 0)
        out = part if i == 0 else out + part
    out = out * (1.0 / total)
    for j in range(k // LANES):
        packed_ref[valid + j * m : valid + (j + 1) * m, :] = out[:, j * LANES : (j + 1) * LANES]
    modes_out.wait()


def in_hbm(x):
    return pltpu.with_memory_space_constraint(x, pltpu.HBM)


def head(snapshots, validation, e_rows, w_row, total, rows):
    n, k = snapshots.shape
    m = e_rows.shape[0]
    hbm, vmem = pl.BlockSpec(memory_space=pltpu.HBM), pl.BlockSpec(memory_space=pltpu.VMEM)
    return pl.pallas_call(
        functools.partial(head_kernel, total),
        out_shape=(
            pltpu.VMEM((rows, LANES), F32), pltpu.HBM((m, n), F32),
            pltpu.VMEM((2 * m, k), jnp.bfloat16), pltpu.VMEM((m, LANES), F32),
        ),
        in_specs=[hbm] * 4,
        out_specs=(vmem, hbm, vmem, vmem),
        scratch_shapes=[
            pltpu.VMEM((n, k), F32), pltpu.VMEM((n, k), F32), pltpu.VMEM((m, k), F32), pltpu.VMEM((1, m), F32),
            pltpu.VMEM((m, n), F32), pltpu.SemaphoreType.DMA((7,)),
        ],
        compiler_params=pltpu.CompilerParams(vmem_limit_bytes=24 * 1024 * 1024),
        name="head",
    )(in_hbm(snapshots), in_hbm(validation), in_hbm(e_rows), in_hbm(w_row))


def tail_kernel(packed_ref, e_ref, scale_ref, gram_hbm, train_hbm, valid_hbm, gram, train_ref, sems):
    m, k = train_ref.shape
    half = k // 2
    mixed, cross, valid, diagonal, _ = layout(k, m)
    tiles = half // LANES
    sent = []

    def send(src, dst):
        sent.append(pltpu.make_async_copy(src, dst, sems.at[len(sent)]))
        sent[-1].start()

    for j in range(k // LANES):
        send(packed_ref.at[pl.ds(valid + j * m, m)], valid_hbm.at[:, pl.ds(j * LANES, LANES)])
    get = lambda first, j: packed_ref[first + j * half : first + (j + 1) * half, :]
    square = jnp.concatenate([get(mixed, j) for j in range(tiles)], 1)
    b = jnp.concatenate([get(cross, j) for j in range(tiles)], 1)
    last = jnp.concatenate([packed_ref[diagonal + j : diagonal + j + 1, :] for j in range(tiles)], 1)
    r, col = order(half)
    turned = square.T
    gram[:half, :half] = jnp.where(col >= r, square, turned)
    gram[:half, half:] = b
    send(gram.at[pl.ds(0, half)], gram_hbm.at[pl.ds(0, half)])
    gram[half:, :half] = b.T
    gram[half:, half:] = jnp.where(col < r, square, jnp.where(col == r, jnp.broadcast_to(last, (half, half)), turned))
    send(gram.at[pl.ds(half, half)], gram_hbm.at[pl.ds(half, half)])
    g_high, g_low = split(gram[...])
    both = dot(e_ref[...], g_high, 1, 0)
    train_ref[...] = (both[:m] + both[m:] + dot(e_ref[:m, :], g_low, 1, 0)) * scale_ref[:, :1]
    send(train_ref, train_hbm)
    for copy in sent:
        copy.wait()


def tail(packed, e_both, scales):
    m, k = scales.shape[0], e_both.shape[1]
    hbm, vmem = pl.BlockSpec(memory_space=pltpu.HBM), pl.BlockSpec(memory_space=pltpu.VMEM)
    coef = pltpu.HBM((m, k), F32)
    return pl.pallas_call(
        tail_kernel,
        out_shape=(pltpu.HBM((k, k), F32), coef, coef),
        in_specs=[vmem, vmem, vmem],
        out_specs=(hbm, hbm, hbm),
        scratch_shapes=[pltpu.VMEM((k, k), F32), pltpu.VMEM((m, k), F32), pltpu.SemaphoreType.DMA((k // LANES + 3,))],
        compiler_params=pltpu.CompilerParams(vmem_limit_bytes=16 * 1024 * 1024),
        name="tail",
    )(packed, e_both, scales)


def partners(n, r):
    return [(i, i ^ r) for i in range(n)]


def tree(parts):
    while len(parts) > 1:
        parts = [a + b for a, b in zip(parts[::2], parts[1::2], strict=True)]
    return parts[0]


def direct(n):
    return n <= DIRECT and n & (n - 1) == 0


def reduce_scatter(x, axis):
    n = lax.axis_size(axis)
    if not direct(n):
        return lax.psum_scatter(x, axis)
    me = lax.axis_index(axis)
    parts = [lax.dynamic_index_in_dim(x, me ^ r, 0, False) for r in range(n)]
    return tree([p if r == 0 else lax.ppermute(p, axis, partners(n, r)) for r, p in enumerate(parts)])


def all_reduce(x, axis):
    n = lax.axis_size(axis)
    if not direct(n):
        return lax.psum(x, axis)
    return tree([x if r == 0 else lax.ppermute(x, axis, partners(n, r)) for r in range(n)])


def all_gather(own, outer, inner):
    no, ni = lax.axis_size(outer), lax.axis_size(inner)
    if not (direct(no) and direct(ni)):
        return lax.all_gather(lax.all_gather(own, inner), outer)
    mo, mi = lax.axis_index(outer), lax.axis_index(inner)
    got = [own if r == 0 else lax.ppermute(own, inner, partners(ni, r)) for r in range(ni)]
    out = jnp.zeros((no, ni) + own.shape, own.dtype)
    for r, row in enumerate(got):
        for q in range(no):
            there = row if q == 0 else lax.ppermute(row, outer, partners(no, q))
            out = lax.dynamic_update_slice(out, there[None, None], (mo ^ q, mi ^ r) + (0,) * own.ndim)
    return out


def body(snapshots, validation, eigenvectors, eigenvalues):
    cores, chips = lax.axis_size("core"), lax.axis_size("chip")
    devices = cores * chips * lax.axis_size("plane")
    total = snapshots.shape[0] * devices * 1.0
    k, m = eigenvectors.shape
    piece = -(-layout(k, m)[-1] // (cores * chips * 8)) * 8
    e_rows, w_row = eigenvectors.T, eigenvalues[None, :]

    packed, modes, e_both, scales = head(snapshots, validation, e_rows, w_row, total, cores * chips * piece)
    own = reduce_scatter(packed.reshape(cores, chips, piece, LANES), "core")
    own = reduce_scatter(own, "chip")
    own = all_reduce(own, "plane")
    packed = all_gather(own, "core", "chip").reshape(-1, LANES)
    gram, train_coef, valid_coef = tail(packed, e_both, scales)
    return gram, modes, train_coef, valid_coef


def solution(mesh):
    inner = axes_of(mesh)
    rows = ("plane", "chip", "core")
    in_specs = (P(rows, None), P(rows, None), P(), P())
    out_specs = (P(), P(None, rows), P(), P())
    return jax.shard_map(body, mesh=inner, in_specs=in_specs, out_specs=out_specs, check_vma=False)
```

time: 41.5 us -> 36.6 us (0.88)
  blocking collectives: 10.6 us -> 0 us
  Pallas kernels: 0 us -> 4.42 us
  waiting for transfers between devices: 13.1 us -> 17.4 us
  starting transfers between devices: 9.46 us -> 13.5 us
  matrix products: 3.19 us -> 0 us
  local copies, waits for them, and re-layouts: 3.16 us -> 0.19 us
  other arithmetic: 0.85 us -> 0.1 us
    all_gather x1 -> x0, blocking collectives: 10.6 us -> none  [body(): packed = lax.all_gather(own, ('chip', 'core'), tiled=True)]
    ppermute x0 -> x7, waiting for transfers between devices: none -> 4.64 us  [the longest x3 3.79 us: all_gather(): lax.ppermute(own, inner, partners(ni, r))]
    pallas_call x0 -> x2, Pallas kernels: none -> 4.42 us  [the longest x1 3.2 us: head(): pl.pallas_call(functools.partial(head_kernel, total), out_shape=(pltpu.VM...]
    ppermute x0 -> x7, starting transfers between devices: none -> 4.07 us  [the longest x3 3.55 us: all_gather(): lax.ppermute(own, inner, partners(ni, r))]
    dot_general x4 -> x0, matrix products: 3.19 us -> none  [body(): lax.dot_general(a, b, (dims, ((), ())), precision=p, preferred_element_ty...]
    unnamed x27 -> x0, local copies, waits for them, and re-layouts: 2.59 us -> none
    concatenate x3 -> x0, other arithmetic: 0.76 us -> none  [the longest x1 0.66 us: body(): jnp.concatenate([packed[base + j * m:base + (j + 1) * m] for j in range(b...]
  transfers between devices with their start and end apart: 7 -> 14, of which waited for: 7 -> 11; matrix products, arithmetic and copies ran while one was open for 0% -> 0% of each run, Pallas kernels for 0% -> 0%
where the time goes in v2:
time: 36.6 us; the launch traced here: 36.4 us
  waiting for transfers between devices  17.4 us (48%)
  starting transfers between devices  13.5 us (37%)
  Pallas kernels  4.42 us (12%)
  between operations  0.73 us (2%)
    ppermute x4, waiting for transfers between devices, reduce_scatter(): lax.ppermute(p, axis, partners(n, r))  6.64 us
    ppermute x3, waiting for transfers between devices, all_reduce(): lax.ppermute(x, axis, partners(n, r))  6.16 us
    ppermute x4, starting transfers between devices, reduce_scatter(): lax.ppermute(p, axis, partners(n, r))  5.01 us
    ppermute x3, starting transfers between devices, all_reduce(): lax.ppermute(x, axis, partners(n, r))  4.45 us
    ppermute x3, waiting for transfers between devices, all_gather(): lax.ppermute(own, inner, partners(ni, r))  3.79 us
    ppermute x3, starting transfers between devices, all_gather(): lax.ppermute(own, inner, partners(ni, r))  3.55 us
    pallas_call x1, Pallas kernels, head(): pl.pallas_call(functools.partial(head_kernel, total), out_shape=(pltpu.VM...  3.2 us
    pallas_call x1, Pallas kernels, tail(): pl.pallas_call(tail_kernel, out_shape=(pltpu.HBM((k, k), F32), coef, coef...  1.22 us
  transfers between devices with their start and end apart: 14, of which 11 were waited for; matrix products, arithmetic and copies ran while one was open for 0% of the time, Pallas kernels for 0%

profile of v2, /device:TPU:0, one launch (start us, length us, event | category | flops | bytes accessed | tf_op | source)
XLA Modules:
  0.0 36.4 jit_solution(3398970417698478863)
XLA Ops:
  0.6 3.2 %head.1 = (f32[1344,128]{1,0:T(8,128)S(1)}, f32[64,512]{1,0:T(8,128)}, bf16[128,512]{1,0:T(8,128)(2,1)S(1)}, f32[64,128]{1,0:T(8,128)S(1)}) custom-call(f32[512,512]{1,0:T(8,128)} %s_hbm.1, f32[512,512]{1,0:T(8,128)} %v_hbm.1, f32[64,512]{1,0:T(8,128)} %bitcast.37, f32[1,64]{1,0:T(1,128)} %bitcast.38), custom_call_target="tpu_custom_call" | custom-call | tf_op jit(solution)/shard_map/head/pallas_call | solution.py:123
  3.9 0.6 %collective-permute-start = (f32[4,168,128]{2,1,0:T(8,128)S(1)}, f32[4,168,128]{2,1,0:T(8,128)S(1)}, u32[]{:S(2)}, u32[]{:S(2)}) collective-permute-start(f32[4,168,128]{2,1,0:T(8,128)S(1)} %dynamic-slice_bitcast_fusion), channel_id=1, source_target_pairs={{0,1},{1,0},{2,3},{3,2},{4,5},{5,4},{6,7},{7,6},{8,9},{9,8},{10,11... | collective-permute-start | bytes 1032200 | tf_op jit(solution)/shard_map/ppermute | solution.py:208
  4.4 1.3 %collective-permute-done = f32[4,168,128]{2,1,0:T(8,128)S(1)} collective-permute-done((f32[4,168,128]{2,1,0:T(8,128)S(1)}, f32[4,168,128]{2,1,0:T(8,128)S(1)}, u32[]{:S(2)}, u32[]{:S(2)}) %collective-permute-start) | collective-permute-done | bytes 344096 | tf_op jit(solution)/shard_map/ppermute | solution.py:208
  5.8 2.9 %collective-permute-start.1 = (f32[168,128]{1,0:T(8,128)S(1)}, f32[168,128]{1,0:T(8,128)S(1)}, u32[]{:S(2)}, u32[]{:S(2)}) collective-permute-start(f32[168,128]{1,0:T(8,128)S(1)} %get-tuple-element.22), channel_id=1, source_target_pairs={{0,2},{2,0},{4,6},{6,4},{1,3},{3,1},{5,7},{7,5},{8,10},{10,8},{12,... | collective-permute-start | bytes 258056 | tf_op jit(solution)/shard_map/ppermute | solution.py:208
  8.7 1.5 %collective-permute-start.2 = (f32[168,128]{1,0:T(8,128)S(1)}, f32[168,128]{1,0:T(8,128)S(1)}, u32[]{:S(2)}, u32[]{:S(2)}) collective-permute-start(f32[168,128]{1,0:T(8,128)S(1)} %get-tuple-element.21), channel_id=1, source_target_pairs={{0,4},{2,6},{4,0},{6,2},{1,5},{3,7},{5,1},{7,3},{8,12},{10,14},{12... | collective-permute-start | bytes 258056 | tf_op jit(solution)/shard_map/ppermute | solution.py:208
  10.2 0.0 collective-permute-start.3
  10.3 1.3 %collective-permute-done.1 = f32[168,128]{1,0:T(8,128)S(1)} collective-permute-done((f32[168,128]{1,0:T(8,128)S(1)}, f32[168,128]{1,0:T(8,128)S(1)}, u32[]{:S(2)}, u32[]{:S(2)}) %collective-permute-start.1) | collective-permute-done | bytes 86048 | tf_op jit(solution)/shard_map/ppermute | solution.py:208
  11.6 2.6 %collective-permute-done.2 = f32[168,128]{1,0:T(8,128)S(1)} collective-permute-done((f32[168,128]{1,0:T(8,128)S(1)}, f32[168,128]{1,0:T(8,128)S(1)}, u32[]{:S(2)}, u32[]{:S(2)}) %collective-permute-start.2) | collective-permute-done | bytes 86048 | tf_op jit(solution)/shard_map/ppermute | solution.py:208
  14.1 1.5 %collective-permute-done.3 = f32[168,128]{1,0:T(8,128)S(1)} collective-permute-done((f32[168,128]{1,0:T(8,128)S(1)}, f32[168,128]{1,0:T(8,128)S(1)}, u32[]{:S(2)}, u32[]{:S(2)}) %collective-permute-start.3) | collective-permute-done | bytes 86048 | tf_op jit(solution)/shard_map/ppermute | solution.py:208
  15.7 1.6 %collective-permute-start.4 = (f32[168,128]{1,0:T(8,128)S(1)}, f32[168,128]{1,0:T(8,128)S(1)}, u32[]{:S(2)}, u32[]{:S(2)}) collective-permute-start(f32[168,128]{1,0:T(8,128)S(1)} %fusion), channel_id=1, source_target_pairs={{0,8},{8,0},{16,24},{24,16},{1,9},{9,1},{17,25},{25,17},{2,10},{10... | collective-permute-start | bytes 258056 | tf_op jit(solution)/shard_map/ppermute | solution.py:215
  17.3 2.6 %collective-permute-start.5 = (f32[168,128]{1,0:T(8,128)S(1)}, f32[168,128]{1,0:T(8,128)S(1)}, u32[]{:S(2)}, u32[]{:S(2)}) collective-permute-start(f32[168,128]{1,0:T(8,128)S(1)} %fusion), channel_id=1, source_target_pairs={{0,16},{8,24},{16,0},{24,8},{1,17},{9,25},{17,1},{25,9},{2,18},{10... | collective-permute-start | bytes 258056 | tf_op jit(solution)/shard_map/ppermute | solution.py:215
  19.9 0.2 collective-permute-start.6
  20.1 0.6 %collective-permute-done.4 = f32[168,128]{1,0:T(8,128)S(1)} collective-permute-done((f32[168,128]{1,0:T(8,128)S(1)}, f32[168,128]{1,0:T(8,128)S(1)}, u32[]{:S(2)}, u32[]{:S(2)}) %collective-permute-start.4) | collective-permute-done | bytes 86048 | tf_op jit(solution)/shard_map/ppermute | solution.py:215
  20.7 3.8 %collective-permute-done.5 = f32[168,128]{1,0:T(8,128)S(1)} collective-permute-done((f32[168,128]{1,0:T(8,128)S(1)}, f32[168,128]{1,0:T(8,128)S(1)}, u32[]{:S(2)}, u32[]{:S(2)}) %collective-permute-start.5) | collective-permute-done | bytes 86048 | tf_op jit(solution)/shard_map/ppermute | solution.py:215
  24.5 1.7 %collective-permute-done.6 = f32[168,128]{1,0:T(8,128)S(1)} collective-permute-done((f32[168,128]{1,0:T(8,128)S(1)}, f32[168,128]{1,0:T(8,128)S(1)}, u32[]{:S(2)}, u32[]{:S(2)}) %collective-permute-start.6) | collective-permute-done | bytes 86048 | tf_op jit(solution)/shard_map/ppermute | solution.py:215
  26.3 0.6 %collective-permute-start.8 = (f32[168,128]{1,0:T(8,128)S(1)}, f32[168,128]{1,0:T(8,128)S(1)}, u32[]{:S(2)}, u32[]{:S(2)}) collective-permute-start(f32[168,128]{1,0:T(8,128)S(1)} %get-tuple-element.19), channel_id=1, source_target_pairs={{0,2},{2,0},{4,6},{6,4},{1,3},{3,1},{5,7},{7,5},{8,10},{10,8},{12,... | collective-permute-start | bytes 258056 | tf_op jit(solution)/shard_map/ppermute | solution.py:223
  26.9 0.0 collective-permute-start.7
  26.9 0.9 %collective-permute-start.10 = (f32[168,128]{1,0:T(8,128)S(1)}, f32[168,128]{1,0:T(8,128)S(1)}, u32[]{:S(2)}, u32[]{:S(2)}) collective-permute-start(f32[168,128]{1,0:T(8,128)S(1)} %get-tuple-element.19), channel_id=1, source_target_pairs={{0,4},{2,6},{4,0},{6,2},{1,5},{3,7},{5,1},{7,3},{8,12},{10,14},{12... | collective-permute-start | bytes 258056 | tf_op jit(solution)/shard_map/ppermute | solution.py:223
  27.9 2.0 %collective-permute-start.12 = (f32[168,128]{1,0:T(8,128)S(1)}, f32[168,128]{1,0:T(8,128)S(1)}, u32[]{:S(2)}, u32[]{:S(2)}) collective-permute-start(f32[168,128]{1,0:T(8,128)S(1)} %get-tuple-element.19), channel_id=1, source_target_pairs={{0,6},{2,4},{4,2},{6,0},{1,7},{3,5},{5,3},{7,1},{8,14},{10,12},{12... | collective-permute-start | bytes 258056 | tf_op jit(solution)/shard_map/ppermute | solution.py:223
  29.9 1.0 %collective-permute-done.8 = f32[168,128]{1,0:T(8,128)S(1)} collective-permute-done((f32[168,128]{1,0:T(8,128)S(1)}, f32[168,128]{1,0:T(8,128)S(1)}, u32[]{:S(2)}, u32[]{:S(2)}) %collective-permute-start.8) | collective-permute-done | bytes 86048 | tf_op jit(solution)/shard_map/ppermute | solution.py:223
  30.9 0.0 collective-permute-start.9
  30.9 0.0 collective-permute-done.7
  30.9 2.8 %collective-permute-done.10 = f32[168,128]{1,0:T(8,128)S(1)} collective-permute-done((f32[168,128]{1,0:T(8,128)S(1)}, f32[168,128]{1,0:T(8,128)S(1)}, u32[]{:S(2)}, u32[]{:S(2)}) %collective-permute-start.10) | collective-permute-done | bytes 86048 | tf_op jit(solution)/shard_map/ppermute | solution.py:223
  33.7 0.0 collective-permute-start.11
  33.7 0.0 collective-permute-done.12
  33.7 0.5 %collective-permute-start.13 = (f32[168,128]{1,0:T(8,128)S(1)}, f32[168,128]{1,0:T(8,128)S(1)}, u32[]{:S(2)}, u32[]{:S(2)}) collective-permute-start(f32[168,128]{1,0:T(8,128)S(1)} %collective-permute-done.12), channel_id=1, source_target_pairs={{0,1},{1,0},{2,3},{3,2},{4,5},{5,4},{6,7},{7,6},{8,9},{9,8},{10,11... | collective-permute-start | bytes 258056 | tf_op jit(solution)/shard_map/ppermute | solution.py:227
  34.3 0.0 collective-permute-done.9
  34.3 0.7 %collective-permute-done.11 = f32[168,128]{1,0:T(8,128)S(1)} collective-permute-done((f32[168,128]{1,0:T(8,128)S(1)}, f32[168,128]{1,0:T(8,128)S(1)}, u32[]{:S(2)}, u32[]{:S(2)}) %collective-permute-start.11) | collective-permute-done | bytes 86048 | tf_op jit(solution)/shard_map/ppermute | solution.py:227
  35.1 0.1 collective-permute-done.13
  35.2 1.2 %tail.1 = (f32[512,512]{1,0:T(8,128)}, f32[64,512]{1,0:T(8,128)}, f32[64,512]{1,0:T(8,128)}) custom-call(f32[1344,128]{1,0:T(8,128)S(1)} %bitcast.34, bf16[128,512]{1,0:T(8,128)(2,1)S(1)} %get-tuple-element.12.e_ref, f32[64,128]{1,0:T(8,128)S(1)} %get-tuple-element.13.scale_ref), custom_call_target="tpu_custom_call" | custom-call | tf_op jit(solution)/shard_map/tail/pallas_call | solution.py:177
  (13 shorter events, 0.3 us)
Async XLA Ops:
  3.9 1.8 %collective-permute-start = (f32[4,168,128]{2,1,0:T(8,128)S(1)}, f32[4,168,128]{2,1,0:T(8,128)S(1)}, u32[]{:S(2)}, u32[]{:S(2)}) collective-permute-start(f32[4,168,128]{2,1,0:T(8,128)S(1)} %dynamic-slice_bitcast_fusion), channel_id=1, source_target_pairs={{0,1},{1,0},{2,3},{3,2},{4,5},{5,4},{6,7},{7,6},{8,9},{9,8},{10,11... | collective-permute-start | bytes 1032200 | tf_op jit(solution)/shard_map/ppermute | solution.py:208
  5.8 5.7 %collective-permute-start.1 = (f32[168,128]{1,0:T(8,128)S(1)}, f32[168,128]{1,0:T(8,128)S(1)}, u32[]{:S(2)}, u32[]{:S(2)}) collective-permute-start(f32[168,128]{1,0:T(8,128)S(1)} %get-tuple-element.22), channel_id=1, source_target_pairs={{0,2},{2,0},{4,6},{6,4},{1,3},{3,1},{5,7},{7,5},{8,10},{10,8},{12,... | collective-permute-start | bytes 258056 | tf_op jit(solution)/shard_map/ppermute | solution.py:208
  8.7 5.4 %collective-permute-start.2 = (f32[168,128]{1,0:T(8,128)S(1)}, f32[168,128]{1,0:T(8,128)S(1)}, u32[]{:S(2)}, u32[]{:S(2)}) collective-permute-start(f32[168,128]{1,0:T(8,128)S(1)} %get-tuple-element.21), channel_id=1, source_target_pairs={{0,4},{2,6},{4,0},{6,2},{1,5},{3,7},{5,1},{7,3},{8,12},{10,14},{12... | collective-permute-start | bytes 258056 | tf_op jit(solution)/shard_map/ppermute | solution.py:208
  10.2 5.4 %collective-permute-start.3 = (f32[168,128]{1,0:T(8,128)S(1)}, f32[168,128]{1,0:T(8,128)S(1)}, u32[]{:S(2)}, u32[]{:S(2)}) collective-permute-start(f32[168,128]{1,0:T(8,128)S(1)} %get-tuple-element.20), channel_id=1, source_target_pairs={{0,6},{2,4},{4,2},{6,0},{1,7},{3,5},{5,3},{7,1},{8,14},{10,12},{12... | collective-permute-start | bytes 258056 | tf_op jit(solution)/shard_map/ppermute | solution.py:208
  15.7 5.0 %collective-permute-start.4 = (f32[168,128]{1,0:T(8,128)S(1)}, f32[168,128]{1,0:T(8,128)S(1)}, u32[]{:S(2)}, u32[]{:S(2)}) collective-permute-start(f32[168,128]{1,0:T(8,128)S(1)} %fusion), channel_id=1, source_target_pairs={{0,8},{8,0},{16,24},{24,16},{1,9},{9,1},{17,25},{25,17},{2,10},{10... | collective-permute-start | bytes 258056 | tf_op jit(solution)/shard_map/ppermute | solution.py:215
  17.3 7.2 %collective-permute-start.5 = (f32[168,128]{1,0:T(8,128)S(1)}, f32[168,128]{1,0:T(8,128)S(1)}, u32[]{:S(2)}, u32[]{:S(2)}) collective-permute-start(f32[168,128]{1,0:T(8,128)S(1)} %fusion), channel_id=1, source_target_pairs={{0,16},{8,24},{16,0},{24,8},{1,17},{9,25},{17,1},{25,9},{2,18},{10... | collective-permute-start | bytes 258056 | tf_op jit(solution)/shard_map/ppermute | solution.py:215
  19.9 6.4 %collective-permute-start.6 = (f32[168,128]{1,0:T(8,128)S(1)}, f32[168,128]{1,0:T(8,128)S(1)}, u32[]{:S(2)}, u32[]{:S(2)}) collective-permute-start(f32[168,128]{1,0:T(8,128)S(1)} %fusion), channel_id=1, source_target_pairs={{0,24},{8,16},{16,8},{24,0},{1,25},{9,17},{17,9},{25,1},{2,26},{10... | collective-permute-start | bytes 258056 | tf_op jit(solution)/shard_map/ppermute | solution.py:215
  26.3 4.5 %collective-permute-start.8 = (f32[168,128]{1,0:T(8,128)S(1)}, f32[168,128]{1,0:T(8,128)S(1)}, u32[]{:S(2)}, u32[]{:S(2)}) collective-permute-start(f32[168,128]{1,0:T(8,128)S(1)} %get-tuple-element.19), channel_id=1, source_target_pairs={{0,2},{2,0},{4,6},{6,4},{1,3},{3,1},{5,7},{7,5},{8,10},{10,8},{12,... | collective-permute-start | bytes 258056 | tf_op jit(solution)/shard_map/ppermute | solution.py:223
  26.9 4.0 %collective-permute-start.7 = (f32[168,128]{1,0:T(8,128)S(1)}, f32[168,128]{1,0:T(8,128)S(1)}, u32[]{:S(2)}, u32[]{:S(2)}) collective-permute-start(f32[168,128]{1,0:T(8,128)S(1)} %get-tuple-element.19), channel_id=1, source_target_pairs={{0,1},{1,0},{2,3},{3,2},{4,5},{5,4},{6,7},{7,6},{8,9},{9,8},{10,11... | collective-permute-start | bytes 258056 | tf_op jit(solution)/shard_map/ppermute | solution.py:227
  26.9 6.8 %collective-permute-start.10 = (f32[168,128]{1,0:T(8,128)S(1)}, f32[168,128]{1,0:T(8,128)S(1)}, u32[]{:S(2)}, u32[]{:S(2)}) collective-permute-start(f32[168,128]{1,0:T(8,128)S(1)} %get-tuple-element.19), channel_id=1, source_target_pairs={{0,4},{2,6},{4,0},{6,2},{1,5},{3,7},{5,1},{7,3},{8,12},{10,14},{12... | collective-permute-start | bytes 258056 | tf_op jit(solution)/shard_map/ppermute | solution.py:223
  27.9 5.8 %collective-permute-start.12 = (f32[168,128]{1,0:T(8,128)S(1)}, f32[168,128]{1,0:T(8,128)S(1)}, u32[]{:S(2)}, u32[]{:S(2)}) collective-permute-start(f32[168,128]{1,0:T(8,128)S(1)} %get-tuple-element.19), channel_id=1, source_target_pairs={{0,6},{2,4},{4,2},{6,0},{1,7},{3,5},{5,3},{7,1},{8,14},{10,12},{12... | collective-permute-start | bytes 258056 | tf_op jit(solution)/shard_map/ppermute | solution.py:223
  30.9 3.4 %collective-permute-start.9 = (f32[168,128]{1,0:T(8,128)S(1)}, f32[168,128]{1,0:T(8,128)S(1)}, u32[]{:S(2)}, u32[]{:S(2)}) collective-permute-start(f32[168,128]{1,0:T(8,128)S(1)} %collective-permute-done.8), channel_id=1, source_target_pairs={{0,1},{1,0},{2,3},{3,2},{4,5},{5,4},{6,7},{7,6},{8,9},{9,8},{10,11... | collective-permute-start | bytes 258056 | tf_op jit(solution)/shard_map/ppermute | solution.py:227
  33.7 1.3 %collective-permute-start.11 = (f32[168,128]{1,0:T(8,128)S(1)}, f32[168,128]{1,0:T(8,128)S(1)}, u32[]{:S(2)}, u32[]{:S(2)}) collective-permute-start(f32[168,128]{1,0:T(8,128)S(1)} %collective-permute-done.10), channel_id=1, source_target_pairs={{0,1},{1,0},{2,3},{3,2},{4,5},{5,4},{6,7},{7,6},{8,9},{9,8},{10,11... | collective-permute-start | bytes 258056 | tf_op jit(solution)/shard_map/ppermute | solution.py:227
  33.7 1.4 %collective-permute-start.13 = (f32[168,128]{1,0:T(8,128)S(1)}, f32[168,128]{1,0:T(8,128)S(1)}, u32[]{:S(2)}, u32[]{:S(2)}) collective-permute-start(f32[168,128]{1,0:T(8,128)S(1)} %collective-permute-done.12), channel_id=1, source_target_pairs={{0,1},{1,0},{2,3},{3,2},{4,5},{5,4},{6,7},{7,6},{8,9},{9,8},{10,11... | collective-permute-start | bytes 258056 | tf_op jit(solution)/shard_map/ppermute | solution.py:227

commit v3 on v2

--- a/solution.py
+++ b/solution.py
@@ -7,6 +7,7 @@
 from jax.experimental.pallas import tpu as pltpu
 from jax.sharding import Mesh, PartitionSpec as P
 
+
 LANES = 128
 DIRECT = 4
 F32 = jnp.float32
@@ -53,7 +54,7 @@
     n, k = s_buf.shape
     m = e_buf.shape[0]
     half, step = k // 2, n // 2
-    mixed, cross, valid, diagonal, rows = layout(k, m)
+    mixed, cross, valid, diagonal, _ = layout(k, m)
     copies = []
     halves = [pl.ds(i * step, step) for i in range(2)]
     for src, buf in [
@@ -199,20 +200,24 @@
     return n <= DIRECT and n & (n - 1) == 0
 
 
+def permute(x, axis, r):
+    return lax.ppermute(x, axis, partners(lax.axis_size(axis), r))
+
+
 def reduce_scatter(x, axis):
     n = lax.axis_size(axis)
     if not direct(n):
         return lax.psum_scatter(x, axis)
     me = lax.axis_index(axis)
     parts = [lax.dynamic_index_in_dim(x, me ^ r, 0, False) for r in range(n)]
-    return tree([p if r == 0 else lax.ppermute(p, axis, partners(n, r)) for r, p in enumerate(parts)])
+    return tree([p if r == 0 else permute(p, axis, r) for r, p in enumerate(parts)])
 
 
 def all_reduce(x, axis):
     n = lax.axis_size(axis)
     if not direct(n):
         return lax.psum(x, axis)
-    return tree([x if r == 0 else lax.ppermute(x, axis, partners(n, r)) for r in range(n)])
+    return tree([x if r == 0 else permute(x, axis, r) for r in range(n)])
 
 
 def all_gather(own, outer, inner):
@@ -220,7 +225,7 @@
     if not (direct(no) and direct(ni)):
         return lax.all_gather(lax.all_gather(own, inner), outer)
     mo, mi = lax.axis_index(outer), lax.axis_index(inner)
-    got = [own if r == 0 else lax.ppermute(own, inner, partners(ni, r)) for r in range(ni)]
+    got = [own if r == 0 else permute(own, inner, r) for r in range(ni)]
     out = jnp.zeros((no, ni) + own.shape, own.dtype)
     for r, row in enumerate(got):
         for q in range(no):
@@ -251,4 +256,7 @@
     rows = ("plane", "chip", "core")
     in_specs = (P(rows, None), P(rows, None), P(), P())
     out_specs = (P(), P(None, rows), P(), P())
-    return jax.shard_map(body, mesh=inner, in_specs=in_specs, out_specs=out_specs, check_vma=False)
+    step = jax.shard_map(body, mesh=inner, in_specs=in_specs, out_specs=out_specs, check_vma=False)
+    if not all(direct(n) for n in inner.devices.shape):
+        return step
+    return step

time: 36.6 us -> 36.6 us (level)
  no operation moved by 1% of the time
where the time goes in v3:
time: 36.6 us; the launch traced here: 36.4 us
  waiting for transfers between devices  17.4 us (48%)
  starting transfers between devices  13.5 us (37%)
  Pallas kernels  4.42 us (12%)
  between operations  0.73 us (2%)
    ppermute x10, waiting for transfers between devices, permute(): return lax.ppermute(x, axis, partners(lax.axis_size(axis), r))  16.6 us
    ppermute x10, starting transfers between devices, permute(): return lax.ppermute(x, axis, partners(lax.axis_size(axis), r))  13 us
    pallas_call x1, Pallas kernels, head(): pl.pallas_call(functools.partial(head_kernel, total), out_shape=(pltpu.VM...  3.2 us
    pallas_call x1, Pallas kernels, tail(): pl.pallas_call(tail_kernel, out_shape=(pltpu.HBM((k, k), F32), coef, coef...  1.22 us
    ppermute x4, waiting for transfers between devices, all_gather(): there = row if q == 0 else lax.ppermute(row, outer, partners(no, q))  0.86 us
  transfers between devices with their start and end apart: 14, of which 11 were waited for; matrix products, arithmetic and copies ran while one was open for 0% of the time, Pallas kernels for 0%

profile of v3, /device:TPU:0, one launch (start us, length us, event | category | flops | bytes accessed | tf_op | source)
XLA Modules:
  0.0 36.4 jit_solution(3398970417698478863)
XLA Ops:
  0.6 3.2 %head.1 = (f32[1344,128]{1,0:T(8,128)S(1)}, f32[64,512]{1,0:T(8,128)}, bf16[128,512]{1,0:T(8,128)(2,1)S(1)}, f32[64,128]{1,0:T(8,128)S(1)}) custom-call(f32[512,512]{1,0:T(8,128)} %s_hbm.1, f32[512,512]{1,0:T(8,128)} %v_hbm.1, f32[64,512]{1,0:T(8,128)} %bitcast.37, f32[1,64]{1,0:T(1,128)} %bitcast.38), custom_call_target="tpu_custom_call" | custom-call | tf_op jit(solution)/shard_map/head/pallas_call | solution.py:124
  3.9 0.6 %collective-permute-start = (f32[4,168,128]{2,1,0:T(8,128)S(1)}, f32[4,168,128]{2,1,0:T(8,128)S(1)}, u32[]{:S(2)}, u32[]{:S(2)}) collective-permute-start(f32[4,168,128]{2,1,0:T(8,128)S(1)} %dynamic-slice_bitcast_fusion), channel_id=1, source_target_pairs={{0,1},{1,0},{2,3},{3,2},{4,5},{5,4},{6,7},{7,6},{8,9},{9,8},{10,11... | collective-permute-start | bytes 1032200 | tf_op jit(solution)/shard_map/ppermute | solution.py:204
  4.4 1.3 %collective-permute-done = f32[4,168,128]{2,1,0:T(8,128)S(1)} collective-permute-done((f32[4,168,128]{2,1,0:T(8,128)S(1)}, f32[4,168,128]{2,1,0:T(8,128)S(1)}, u32[]{:S(2)}, u32[]{:S(2)}) %collective-permute-start) | collective-permute-done | bytes 344096 | tf_op jit(solution)/shard_map/ppermute | solution.py:204
  5.8 2.9 %collective-permute-start.1 = (f32[168,128]{1,0:T(8,128)S(1)}, f32[168,128]{1,0:T(8,128)S(1)}, u32[]{:S(2)}, u32[]{:S(2)}) collective-permute-start(f32[168,128]{1,0:T(8,128)S(1)} %get-tuple-element.22), channel_id=1, source_target_pairs={{0,2},{2,0},{4,6},{6,4},{1,3},{3,1},{5,7},{7,5},{8,10},{10,8},{12,... | collective-permute-start | bytes 258056 | tf_op jit(solution)/shard_map/ppermute | solution.py:204
  8.7 1.5 %collective-permute-start.2 = (f32[168,128]{1,0:T(8,128)S(1)}, f32[168,128]{1,0:T(8,128)S(1)}, u32[]{:S(2)}, u32[]{:S(2)}) collective-permute-start(f32[168,128]{1,0:T(8,128)S(1)} %get-tuple-element.21), channel_id=1, source_target_pairs={{0,4},{2,6},{4,0},{6,2},{1,5},{3,7},{5,1},{7,3},{8,12},{10,14},{12... | collective-permute-start | bytes 258056 | tf_op jit(solution)/shard_map/ppermute | solution.py:204
  10.2 0.0 collective-permute-start.3
  10.3 1.3 %collective-permute-done.1 = f32[168,128]{1,0:T(8,128)S(1)} collective-permute-done((f32[168,128]{1,0:T(8,128)S(1)}, f32[168,128]{1,0:T(8,128)S(1)}, u32[]{:S(2)}, u32[]{:S(2)}) %collective-permute-start.1) | collective-permute-done | bytes 86048 | tf_op jit(solution)/shard_map/ppermute | solution.py:204
  11.6 2.6 %collective-permute-done.2 = f32[168,128]{1,0:T(8,128)S(1)} collective-permute-done((f32[168,128]{1,0:T(8,128)S(1)}, f32[168,128]{1,0:T(8,128)S(1)}, u32[]{:S(2)}, u32[]{:S(2)}) %collective-permute-start.2) | collective-permute-done | bytes 86048 | tf_op jit(solution)/shard_map/ppermute | solution.py:204
  14.1 1.5 %collective-permute-done.3 = f32[168,128]{1,0:T(8,128)S(1)} collective-permute-done((f32[168,128]{1,0:T(8,128)S(1)}, f32[168,128]{1,0:T(8,128)S(1)}, u32[]{:S(2)}, u32[]{:S(2)}) %collective-permute-start.3) | collective-permute-done | bytes 86048 | tf_op jit(solution)/shard_map/ppermute | solution.py:204
  15.7 1.6 %collective-permute-start.4 = (f32[168,128]{1,0:T(8,128)S(1)}, f32[168,128]{1,0:T(8,128)S(1)}, u32[]{:S(2)}, u32[]{:S(2)}) collective-permute-start(f32[168,128]{1,0:T(8,128)S(1)} %fusion), channel_id=1, source_target_pairs={{0,8},{8,0},{16,24},{24,16},{1,9},{9,1},{17,25},{25,17},{2,10},{10... | collective-permute-start | bytes 258056 | tf_op jit(solution)/shard_map/ppermute | solution.py:204
  17.3 2.6 %collective-permute-start.5 = (f32[168,128]{1,0:T(8,128)S(1)}, f32[168,128]{1,0:T(8,128)S(1)}, u32[]{:S(2)}, u32[]{:S(2)}) collective-permute-start(f32[168,128]{1,0:T(8,128)S(1)} %fusion), channel_id=1, source_target_pairs={{0,16},{8,24},{16,0},{24,8},{1,17},{9,25},{17,1},{25,9},{2,18},{10... | collective-permute-start | bytes 258056 | tf_op jit(solution)/shard_map/ppermute | solution.py:204
  19.9 0.2 collective-permute-start.6
  20.1 0.6 %collective-permute-done.4 = f32[168,128]{1,0:T(8,128)S(1)} collective-permute-done((f32[168,128]{1,0:T(8,128)S(1)}, f32[168,128]{1,0:T(8,128)S(1)}, u32[]{:S(2)}, u32[]{:S(2)}) %collective-permute-start.4) | collective-permute-done | bytes 86048 | tf_op jit(solution)/shard_map/ppermute | solution.py:204
  20.7 3.8 %collective-permute-done.5 = f32[168,128]{1,0:T(8,128)S(1)} collective-permute-done((f32[168,128]{1,0:T(8,128)S(1)}, f32[168,128]{1,0:T(8,128)S(1)}, u32[]{:S(2)}, u32[]{:S(2)}) %collective-permute-start.5) | collective-permute-done | bytes 86048 | tf_op jit(solution)/shard_map/ppermute | solution.py:204
  24.5 1.7 %collective-permute-done.6 = f32[168,128]{1,0:T(8,128)S(1)} collective-permute-done((f32[168,128]{1,0:T(8,128)S(1)}, f32[168,128]{1,0:T(8,128)S(1)}, u32[]{:S(2)}, u32[]{:S(2)}) %collective-permute-start.6) | collective-permute-done | bytes 86048 | tf_op jit(solution)/shard_map/ppermute | solution.py:204
  26.3 0.6 %collective-permute-start.8 = (f32[168,128]{1,0:T(8,128)S(1)}, f32[168,128]{1,0:T(8,128)S(1)}, u32[]{:S(2)}, u32[]{:S(2)}) collective-permute-start(f32[168,128]{1,0:T(8,128)S(1)} %get-tuple-element.19), channel_id=1, source_target_pairs={{0,2},{2,0},{4,6},{6,4},{1,3},{3,1},{5,7},{7,5},{8,10},{10,8},{12,... | collective-permute-start | bytes 258056 | tf_op jit(solution)/shard_map/ppermute | solution.py:204
  26.9 0.0 collective-permute-start.7
  26.9 0.9 %collective-permute-start.10 = (f32[168,128]{1,0:T(8,128)S(1)}, f32[168,128]{1,0:T(8,128)S(1)}, u32[]{:S(2)}, u32[]{:S(2)}) collective-permute-start(f32[168,128]{1,0:T(8,128)S(1)} %get-tuple-element.19), channel_id=1, source_target_pairs={{0,4},{2,6},{4,0},{6,2},{1,5},{3,7},{5,1},{7,3},{8,12},{10,14},{12... | collective-permute-start | bytes 258056 | tf_op jit(solution)/shard_map/ppermute | solution.py:204
  27.9 2.0 %collective-permute-start.12 = (f32[168,128]{1,0:T(8,128)S(1)}, f32[168,128]{1,0:T(8,128)S(1)}, u32[]{:S(2)}, u32[]{:S(2)}) collective-permute-start(f32[168,128]{1,0:T(8,128)S(1)} %get-tuple-element.19), channel_id=1, source_target_pairs={{0,6},{2,4},{4,2},{6,0},{1,7},{3,5},{5,3},{7,1},{8,14},{10,12},{12... | collective-permute-start | bytes 258056 | tf_op jit(solution)/shard_map/ppermute | solution.py:204
  29.9 1.0 %collective-permute-done.8 = f32[168,128]{1,0:T(8,128)S(1)} collective-permute-done((f32[168,128]{1,0:T(8,128)S(1)}, f32[168,128]{1,0:T(8,128)S(1)}, u32[]{:S(2)}, u32[]{:S(2)}) %collective-permute-start.8) | collective-permute-done | bytes 86048 | tf_op jit(solution)/shard_map/ppermute | solution.py:204
  30.9 0.0 collective-permute-start.9
  30.9 0.0 collective-permute-done.7
  30.9 2.8 %collective-permute-done.10 = f32[168,128]{1,0:T(8,128)S(1)} collective-permute-done((f32[168,128]{1,0:T(8,128)S(1)}, f32[168,128]{1,0:T(8,128)S(1)}, u32[]{:S(2)}, u32[]{:S(2)}) %collective-permute-start.10) | collective-permute-done | bytes 86048 | tf_op jit(solution)/shard_map/ppermute | solution.py:204
  33.7 0.0 collective-permute-start.11
  33.7 0.0 collective-permute-done.12
  33.7 0.5 %collective-permute-start.13 = (f32[168,128]{1,0:T(8,128)S(1)}, f32[168,128]{1,0:T(8,128)S(1)}, u32[]{:S(2)}, u32[]{:S(2)}) collective-permute-start(f32[168,128]{1,0:T(8,128)S(1)} %collective-permute-done.12), channel_id=1, source_target_pairs={{0,1},{1,0},{2,3},{3,2},{4,5},{5,4},{6,7},{7,6},{8,9},{9,8},{10,11... | collective-permute-start | bytes 258056 | tf_op jit(solution)/shard_map/ppermute | solution.py:232
  34.3 0.0 collective-permute-done.9
  34.3 0.7 %collective-permute-done.11 = f32[168,128]{1,0:T(8,128)S(1)} collective-permute-done((f32[168,128]{1,0:T(8,128)S(1)}, f32[168,128]{1,0:T(8,128)S(1)}, u32[]{:S(2)}, u32[]{:S(2)}) %collective-permute-start.11) | collective-permute-done | bytes 86048 | tf_op jit(solution)/shard_map/ppermute | solution.py:232
  35.1 0.1 collective-permute-done.13
  35.2 1.2 %tail.1 = (f32[512,512]{1,0:T(8,128)}, f32[64,512]{1,0:T(8,128)}, f32[64,512]{1,0:T(8,128)}) custom-call(f32[1344,128]{1,0:T(8,128)S(1)} %bitcast.34, bf16[128,512]{1,0:T(8,128)(2,1)S(1)} %get-tuple-element.12.e_ref, f32[64,128]{1,0:T(8,128)S(1)} %get-tuple-element.13.scale_ref), custom_call_target="tpu_custom_call" | custom-call | tf_op jit(solution)/shard_map/tail/pallas_call | solution.py:178
  (13 shorter events, 0.3 us)
Async XLA Ops:
  3.9 1.8 %collective-permute-start = (f32[4,168,128]{2,1,0:T(8,128)S(1)}, f32[4,168,128]{2,1,0:T(8,128)S(1)}, u32[]{:S(2)}, u32[]{:S(2)}) collective-permute-start(f32[4,168,128]{2,1,0:T(8,128)S(1)} %dynamic-slice_bitcast_fusion), channel_id=1, source_target_pairs={{0,1},{1,0},{2,3},{3,2},{4,5},{5,4},{6,7},{7,6},{8,9},{9,8},{10,11... | collective-permute-start | bytes 1032200 | tf_op jit(solution)/shard_map/ppermute | solution.py:204
  5.8 5.7 %collective-permute-start.1 = (f32[168,128]{1,0:T(8,128)S(1)}, f32[168,128]{1,0:T(8,128)S(1)}, u32[]{:S(2)}, u32[]{:S(2)}) collective-permute-start(f32[168,128]{1,0:T(8,128)S(1)} %get-tuple-element.22), channel_id=1, source_target_pairs={{0,2},{2,0},{4,6},{6,4},{1,3},{3,1},{5,7},{7,5},{8,10},{10,8},{12,... | collective-permute-start | bytes 258056 | tf_op jit(solution)/shard_map/ppermute | solution.py:204
  8.7 5.4 %collective-permute-start.2 = (f32[168,128]{1,0:T(8,128)S(1)}, f32[168,128]{1,0:T(8,128)S(1)}, u32[]{:S(2)}, u32[]{:S(2)}) collective-permute-start(f32[168,128]{1,0:T(8,128)S(1)} %get-tuple-element.21), channel_id=1, source_target_pairs={{0,4},{2,6},{4,0},{6,2},{1,5},{3,7},{5,1},{7,3},{8,12},{10,14},{12... | collective-permute-start | bytes 258056 | tf_op jit(solution)/shard_map/ppermute | solution.py:204
  10.2 5.4 %collective-permute-start.3 = (f32[168,128]{1,0:T(8,128)S(1)}, f32[168,128]{1,0:T(8,128)S(1)}, u32[]{:S(2)}, u32[]{:S(2)}) collective-permute-start(f32[168,128]{1,0:T(8,128)S(1)} %get-tuple-element.20), channel_id=1, source_target_pairs={{0,6},{2,4},{4,2},{6,0},{1,7},{3,5},{5,3},{7,1},{8,14},{10,12},{12... | collective-permute-start | bytes 258056 | tf_op jit(solution)/shard_map/ppermute | solution.py:204
  15.7 5.0 %collective-permute-start.4 = (f32[168,128]{1,0:T(8,128)S(1)}, f32[168,128]{1,0:T(8,128)S(1)}, u32[]{:S(2)}, u32[]{:S(2)}) collective-permute-start(f32[168,128]{1,0:T(8,128)S(1)} %fusion), channel_id=1, source_target_pairs={{0,8},{8,0},{16,24},{24,16},{1,9},{9,1},{17,25},{25,17},{2,10},{10... | collective-permute-start | bytes 258056 | tf_op jit(solution)/shard_map/ppermute | solution.py:204
  17.3 7.2 %collective-permute-start.5 = (f32[168,128]{1,0:T(8,128)S(1)}, f32[168,128]{1,0:T(8,128)S(1)}, u32[]{:S(2)}, u32[]{:S(2)}) collective-permute-start(f32[168,128]{1,0:T(8,128)S(1)} %fusion), channel_id=1, source_target_pairs={{0,16},{8,24},{16,0},{24,8},{1,17},{9,25},{17,1},{25,9},{2,18},{10... | collective-permute-start | bytes 258056 | tf_op jit(solution)/shard_map/ppermute | solution.py:204
  19.9 6.4 %collective-permute-start.6 = (f32[168,128]{1,0:T(8,128)S(1)}, f32[168,128]{1,0:T(8,128)S(1)}, u32[]{:S(2)}, u32[]{:S(2)}) collective-permute-start(f32[168,128]{1,0:T(8,128)S(1)} %fusion), channel_id=1, source_target_pairs={{0,24},{8,16},{16,8},{24,0},{1,25},{9,17},{17,9},{25,1},{2,26},{10... | collective-permute-start | bytes 258056 | tf_op jit(solution)/shard_map/ppermute | solution.py:204
  26.3 4.5 %collective-permute-start.8 = (f32[168,128]{1,0:T(8,128)S(1)}, f32[168,128]{1,0:T(8,128)S(1)}, u32[]{:S(2)}, u32[]{:S(2)}) collective-permute-start(f32[168,128]{1,0:T(8,128)S(1)} %get-tuple-element.19), channel_id=1, source_target_pairs={{0,2},{2,0},{4,6},{6,4},{1,3},{3,1},{5,7},{7,5},{8,10},{10,8},{12,... | collective-permute-start | bytes 258056 | tf_op jit(solution)/shard_map/ppermute | solution.py:204
  26.9 4.0 %collective-permute-start.7 = (f32[168,128]{1,0:T(8,128)S(1)}, f32[168,128]{1,0:T(8,128)S(1)}, u32[]{:S(2)}, u32[]{:S(2)}) collective-permute-start(f32[168,128]{1,0:T(8,128)S(1)} %get-tuple-element.19), channel_id=1, source_target_pairs={{0,1},{1,0},{2,3},{3,2},{4,5},{5,4},{6,7},{7,6},{8,9},{9,8},{10,11... | collective-permute-start | bytes 258056 | tf_op jit(solution)/shard_map/ppermute | solution.py:232
  26.9 6.8 %collective-permute-start.10 = (f32[168,128]{1,0:T(8,128)S(1)}, f32[168,128]{1,0:T(8,128)S(1)}, u32[]{:S(2)}, u32[]{:S(2)}) collective-permute-start(f32[168,128]{1,0:T(8,128)S(1)} %get-tuple-element.19), channel_id=1, source_target_pairs={{0,4},{2,6},{4,0},{6,2},{1,5},{3,7},{5,1},{7,3},{8,12},{10,14},{12... | collective-permute-start | bytes 258056 | tf_op jit(solution)/shard_map/ppermute | solution.py:204
  27.9 5.8 %collective-permute-start.12 = (f32[168,128]{1,0:T(8,128)S(1)}, f32[168,128]{1,0:T(8,128)S(1)}, u32[]{:S(2)}, u32[]{:S(2)}) collective-permute-start(f32[168,128]{1,0:T(8,128)S(1)} %get-tuple-element.19), channel_id=1, source_target_pairs={{0,6},{2,4},{4,2},{6,0},{1,7},{3,5},{5,3},{7,1},{8,14},{10,12},{12... | collective-permute-start | bytes 258056 | tf_op jit(solution)/shard_map/ppermute | solution.py:204
  30.9 3.4 %collective-permute-start.9 = (f32[168,128]{1,0:T(8,128)S(1)}, f32[168,128]{1,0:T(8,128)S(1)}, u32[]{:S(2)}, u32[]{:S(2)}) collective-permute-start(f32[168,128]{1,0:T(8,128)S(1)} %collective-permute-done.8), channel_id=1, source_target_pairs={{0,1},{1,0},{2,3},{3,2},{4,5},{5,4},{6,7},{7,6},{8,9},{9,8},{10,11... | collective-permute-start | bytes 258056 | tf_op jit(solution)/shard_map/ppermute | solution.py:232
  33.7 1.3 %collective-permute-start.11 = (f32[168,128]{1,0:T(8,128)S(1)}, f32[168,128]{1,0:T(8,128)S(1)}, u32[]{:S(2)}, u32[]{:S(2)}) collective-permute-start(f32[168,128]{1,0:T(8,128)S(1)} %collective-permute-done.10), channel_id=1, source_target_pairs={{0,1},{1,0},{2,3},{3,2},{4,5},{5,4},{6,7},{7,6},{8,9},{9,8},{10,11... | collective-permute-start | bytes 258056 | tf_op jit(solution)/shard_map/ppermute | solution.py:232
  33.7 1.4 %collective-permute-start.13 = (f32[168,128]{1,0:T(8,128)S(1)}, f32[168,128]{1,0:T(8,128)S(1)}, u32[]{:S(2)}, u32[]{:S(2)}) collective-permute-start(f32[168,128]{1,0:T(8,128)S(1)} %collective-permute-done.12), channel_id=1, source_target_pairs={{0,1},{1,0},{2,3},{3,2},{4,5},{5,4},{6,7},{7,6},{8,9},{9,8},{10,11... | collective-permute-start | bytes 258056 | tf_op jit(solution)/shard_map/ppermute | solution.py:232

commit v4 on v3

v4 whole, which is shorter than its diff:
```python
import functools

import jax
import jax.numpy as jnp
from jax import lax
from jax.experimental import pallas as pl
from jax.experimental.pallas import tpu as pltpu
from jax.sharding import Mesh, PartitionSpec as P


LANES = 128
DIRECT = 4
F32 = jnp.float32


def axes_of(mesh):
    devices = list(mesh.devices.flat)
    cores = len({d.core_on_chip for d in devices})
    planes = len({d.coords[2] for d in devices})
    chips = len(devices) // (cores * planes)
    return Mesh(mesh.devices.reshape(planes, chips, cores), ("plane", "chip", "core"))


def layout(k, m):
    half = k // 2
    square = half * half // LANES
    mixed, cross, valid = 0, square, 2 * square
    diagonal = valid + m * k // LANES
    return mixed, cross, valid, diagonal, diagonal + half // LANES


def split(x):
    high = x.astype(jnp.bfloat16)
    return high, (x - high.astype(F32)).astype(jnp.bfloat16)


def dot(a, b, ca, cb):
    return lax.dot_general(a, b, (((ca,), (cb,)), ((), ())), preferred_element_type=F32)


def column(row, m):
    r, c = (lax.broadcasted_iota(jnp.int32, (m, m), d) for d in (0, 1))
    return jnp.sum(jnp.where(r == c, jnp.broadcast_to(row, (m, m)), 0.0), axis=1, keepdims=True)


def order(half):
    r, c = (lax.broadcasted_iota(jnp.int32, (half, half), d) for d in (0, 1))
    return r, c


def head_kernel(
    total, s_hbm, v_hbm, e_hbm, w_hbm, packed_ref, modes_ref, e_out, scale_out, s_buf, v_buf, e_buf, w_buf, sems
):
    _, k = s_buf.shape
    m = e_buf.shape[0]
    half = k // 2
    mixed, cross, valid, diagonal, _ = layout(k, m)
    copies = []
    for src, buf in [(e_hbm, e_buf), (w_hbm, w_buf), (s_hbm, s_buf), (v_hbm, v_buf)]:
        copies.append(pltpu.make_async_copy(src, buf, sems.at[len(copies)]))
        copies[-1].start()
    for copy in copies[:2]:
        copy.wait()
    scales = column(lax.rsqrt(w_buf[...]), m)
    e_high, e_low = split(e_buf[...])
    e_both = jnp.concatenate([e_high, e_low], 0)
    e_out[...] = e_both
    scale_out[...] = jnp.broadcast_to(scales, scale_out.shape)
    for copy in copies[2:]:
        copy.wait()
    high, low = split(s_buf[...])
    both = dot(high, e_both, 1, 1)
    modes = (both[:, :m] + both[:, m:] + dot(low, e_high, 1, 1)).T * scales
    modes_ref[...] = modes
    ha, hb, la, lb = high[:, :half], high[:, half:], low[:, :half], low[:, half:]
    xa, xb, xc = dot(ha, la, 0, 0), dot(hb, la, 0, 0), dot(hb, lb, 0, 0)
    a = dot(ha, ha, 0, 0) + (xa + xa.T)
    b = dot(ha, hb, 0, 0) + (dot(ha, lb, 0, 0) + xb.T)
    c = dot(hb, hb, 0, 0) + (xc + xc.T)
    m_high, m_low = split(modes)
    v_high, v_low = split(v_buf[...])
    both = dot(jnp.concatenate([m_high, m_low], 0), v_high, 1, 0)
    out = (both[:m] + both[m:] + dot(m_high, v_low, 1, 0)) * (1.0 / total)
    r, col = order(half)
    square = jnp.where(col >= r, a, c) * (1.0 / total)
    b = b * (1.0 / total)
    last = jnp.sum(jnp.where(col == r, c, 0.0), axis=0, keepdims=True) * (1.0 / total)
    for j in range(half // LANES):
        lanes = slice(j * LANES, (j + 1) * LANES)
        packed_ref[mixed + j * half : mixed + (j + 1) * half, :] = square[:, lanes]
        packed_ref[cross + j * half : cross + (j + 1) * half, :] = b[:, lanes]
    pad = packed_ref.shape[0] - diagonal
    packed_ref[diagonal:, :] = jnp.concatenate(
        [last[:, j * LANES : (j + 1) * LANES] for j in range(half // LANES)]
        + [jnp.zeros((pad - half // LANES, LANES), F32)], 0
    )
    for j in range(k // LANES):
        packed_ref[valid + j * m : valid + (j + 1) * m, :] = out[:, j * LANES : (j + 1) * LANES]


def in_hbm(x):
    return pltpu.with_memory_space_constraint(x, pltpu.HBM)


def head(snapshots, validation, e_rows, w_row, total, rows):
    n, k = snapshots.shape
    m = e_rows.shape[0]
    hbm, vmem = pl.BlockSpec(memory_space=pltpu.HBM), pl.BlockSpec(memory_space=pltpu.VMEM)
    return pl.pallas_call(
        functools.partial(head_kernel, total),
        out_shape=(
            pltpu.VMEM((rows, LANES), F32), pltpu.VMEM((m, n), F32),
            pltpu.VMEM((2 * m, k), jnp.bfloat16), pltpu.VMEM((m, LANES), F32),
        ),
        in_specs=[hbm] * 4,
        out_specs=(vmem,) * 4,
        scratch_shapes=[
            pltpu.VMEM((n, k), F32), pltpu.VMEM((n, k), F32), pltpu.VMEM((m, k), F32), pltpu.VMEM((1, m), F32),
            pltpu.SemaphoreType.DMA((4,)),
        ],
        compiler_params=pltpu.CompilerParams(vmem_limit_bytes=24 * 1024 * 1024),
        name="head",
    )(in_hbm(snapshots), in_hbm(validation), in_hbm(e_rows), in_hbm(w_row))


def tail_kernel(
    packed_ref, modes_ref, e_ref, scale_ref, gram_hbm, modes_hbm, train_hbm, valid_hbm, gram, train_ref, sems
):
    m, k = train_ref.shape
    half = k // 2
    mixed, cross, valid, diagonal, _ = layout(k, m)
    tiles = half // LANES
    first, second = pl.ds(0, half), pl.ds(half, half)
    sent = []

    def send(src, dst):
        sent.append(pltpu.make_async_copy(src, dst, sems.at[len(sent)]))
        sent[-1].start()

    for j in range(tiles):
        at = pl.ds(half + j * LANES, LANES)
        send(packed_ref.at[pl.ds(cross + j * half, half)], gram_hbm.at[first, at])
    get = lambda start, j: packed_ref[start + j * half : start + (j + 1) * half, :]
    square = jnp.concatenate([get(mixed, j) for j in range(tiles)], 1)
    r, col = order(half)
    turned = square.T
    gram[:half, :half] = jnp.where(col >= r, square, turned)
    send(gram.at[first, first], gram_hbm.at[first, first])
    last = jnp.concatenate([packed_ref[diagonal + j : diagonal + j + 1, :] for j in range(tiles)], 1)
    gram[half:, half:] = jnp.where(col < r, square, jnp.where(col == r, jnp.broadcast_to(last, (half, half)), turned))
    send(gram.at[second, second], gram_hbm.at[second, second])
    b = jnp.concatenate([get(cross, j) for j in range(tiles)], 1)
    gram[half:, :half] = b.T
    send(gram.at[second, first], gram_hbm.at[second, first])
    gram[:half, half:] = b
    send(modes_ref, modes_hbm)
    for j in range(k // LANES):
        send(packed_ref.at[pl.ds(valid + j * m, m)], valid_hbm.at[:, pl.ds(j * LANES, LANES)])
    g_high, g_low = split(gram[...])
    both = dot(e_ref[...], g_high, 1, 0)
    train_ref[...] = (both[:m] + both[m:] + dot(e_ref[:m, :], g_low, 1, 0)) * scale_ref[:, :1]
    send(train_ref, train_hbm)
    for copy in sent:
        copy.wait()


def tail(packed, modes, e_both, scales):
    m, k = scales.shape[0], e_both.shape[1]
    hbm, vmem = pl.BlockSpec(memory_space=pltpu.HBM), pl.BlockSpec(memory_space=pltpu.VMEM)
    coef = pltpu.HBM((m, k), F32)
    return pl.pallas_call(
        tail_kernel,
        out_shape=(pltpu.HBM((k, k), F32), pltpu.HBM(modes.shape, F32), coef, coef),
        in_specs=[vmem] * 4,
        out_specs=(hbm,) * 4,
        scratch_shapes=[pltpu.VMEM((k, k), F32), pltpu.VMEM((m, k), F32), pltpu.SemaphoreType.DMA((3 * k // (2 * LANES) + 5,))],
        compiler_params=pltpu.CompilerParams(vmem_limit_bytes=16 * 1024 * 1024),
        name="tail",
    )(packed, modes, e_both, scales)


def partners(n, r):
    return [(i, i ^ r) for i in range(n)]


def tree(parts):
    while len(parts) > 1:
        parts = [a + b for a, b in zip(parts[::2], parts[1::2], strict=True)]
    return parts[0]


def direct(n):
    return n <= DIRECT and n & (n - 1) == 0


def permute(x, axis, r):
    return lax.ppermute(x, axis, partners(lax.axis_size(axis), r))


def reduce_scatter(x):
    cores, chips = x.shape[:2]
    if not (cores == 2 and chips > 1 and direct(chips)):
        return lax.psum_scatter(lax.psum_scatter(x, "core"), "chip")
    core, chip = lax.axis_index("core"), lax.axis_index("chip")
    row = lambda c, r: lax.dynamic_slice(x, (c, chip ^ r) + (0,) * (x.ndim - 2), (1, 1) + x.shape[2:])[0, 0]
    up = lambda rows: permute(jnp.stack([row(1 - core, r) for r in rows]), "core", 1)
    first = row(core, 1) + up([1])[0]
    others = [r for r in range(chips) if r != 1]
    theirs, _ = lax.optimization_barrier((up(others), first))
    parts = [row(core, r) + theirs[i] for i, r in enumerate(others)]
    parts.insert(1, first)
    return tree([p if r == 0 else permute(p, "chip", r) for r, p in enumerate(parts)])


def all_reduce(x, axis):
    n = lax.axis_size(axis)
    if not direct(n):
        return lax.psum(x, axis)
    return tree([x if r == 0 else permute(x, axis, r) for r in range(n)])


def all_gather(own, outer, inner):
    no, ni = lax.axis_size(outer), lax.axis_size(inner)
    if not (direct(no) and direct(ni)):
        return lax.all_gather(lax.all_gather(own, inner), outer)
    mo, mi = lax.axis_index(outer), lax.axis_index(inner)
    got = [own if r == 0 else permute(own, inner, r) for r in range(ni)]
    out = jnp.zeros((no, ni) + own.shape, own.dtype)
    for r, row in enumerate(got):
        for q in range(no):
            there = row if q == 0 else lax.ppermute(row, outer, partners(no, q))
            out = lax.dynamic_update_slice(out, there[None, None], (mo ^ q, mi ^ r) + (0,) * own.ndim)
    return out


def body(snapshots, validation, eigenvectors, eigenvalues):
    cores, chips = lax.axis_size("core"), lax.axis_size("chip")
    devices = cores * chips * lax.axis_size("plane")
    total = snapshots.shape[0] * devices * 1.0
    k, m = eigenvectors.shape
    piece = -(-layout(k, m)[-1] // (cores * chips * 8)) * 8
    e_rows, w_row = eigenvectors.T, eigenvalues[None, :]

    packed, modes, e_both, scales = head(snapshots, validation, e_rows, w_row, total, cores * chips * piece)
    own = reduce_scatter(packed.reshape(cores, chips, piece, LANES))
    own = all_reduce(own, "plane")
    packed = all_gather(own, "core", "chip").reshape(-1, LANES)
    return tail(packed, modes, e_both, scales)


def solution(mesh):
    inner = axes_of(mesh)
    rows = ("plane", "chip", "core")
    in_specs = (P(rows, None), P(rows, None), P(), P())
    out_specs = (P(), P(None, rows), P(), P())
    step = jax.shard_map(body, mesh=inner, in_specs=in_specs, out_specs=out_specs, check_vma=False)
    if not all(direct(n) for n in inner.devices.shape):
        return step
    return step
```

time: 36.6 us -> 36.9 us (level)
  waiting for transfers between devices: 17.4 us -> 18.2 us
  Pallas kernels: 4.42 us -> 4.04 us
    ppermute x4, starting transfers between devices: 0.52 us -> 0.01 us  [all_gather(): there = row if q == 0 else lax.ppermute(row, outer, partners(no, q))]
    ppermute x10 -> x11, starting transfers between devices: 13 us -> 13.5 us  [permute(): return lax.ppermute(x, axis, partners(lax.axis_size(axis), r))]
    pallas_call x1, Pallas kernels: 3.2 us -> 2.77 us  [head(): pl.pallas_call(functools.partial(head_kernel, total), out_shape=(pltpu.VM...]
    ppermute x10 -> x11, waiting for transfers between devices: 16.6 us -> 17 us  [permute(): return lax.ppermute(x, axis, partners(lax.axis_size(axis), r))]
  transfers between devices with their start and end apart: 14 -> 15, of which waited for: 11 -> 10; matrix products, arithmetic and copies ran while one was open for 0% -> 0% of each run, Pallas kernels for 0% -> 0%
where the time goes in v4:
time: 36.9 us; the launch traced here: 36.7 us
  waiting for transfers between devices  18.2 us (49%)
  starting transfers between devices  13.5 us (37%)
  Pallas kernels  4.04 us (11%)
  between operations  0.76 us (2%)
    ppermute x11, waiting for transfers between devices, permute(): return lax.ppermute(x, axis, partners(lax.axis_size(axis), r))  17 us
    ppermute x11, starting transfers between devices, permute(): return lax.ppermute(x, axis, partners(lax.axis_size(axis), r))  13.5 us
    pallas_call x1, Pallas kernels, head(): pl.pallas_call(functools.partial(head_kernel, total), out_shape=(pltpu.VM...  2.77 us
    pallas_call x1, Pallas kernels, tail(): pl.pallas_call(tail_kernel, out_shape=(pltpu.HBM((k, k), F32), pltpu.HBM(...  1.27 us
    ppermute x4, waiting for transfers between devices, all_gather(): there = row if q == 0 else lax.ppermute(row, outer, partners(no, q))  1.19 us
  transfers between devices with their start and end apart: 15, of which 10 were waited for; matrix products, arithmetic and copies ran while one was open for 0% of the time, Pallas kernels for 0%

profile of v4, /device:TPU:0, one launch (start us, length us, event | category | flops | bytes accessed | tf_op | source)
XLA Modules:
  0.0 36.7 jit_solution(12551846778770662642)
XLA Ops:
  0.7 2.8 %head.1 = (f32[1344,128]{1,0:T(8,128)S(1)}, f32[64,512]{1,0:T(8,128)S(1)}, bf16[128,512]{1,0:T(8,128)(2,1)S(1)}, f32[64,128]{1,0:T(8,128)S(1)}) custom-call(f32[512,512]{1,0:T(8,128)} %s_hbm.1, f32[512,512]{1,0:T(8,128)} %v_hbm.1, f32[64,512]{1,0:T(8,128)} %bitcast.53, f32[1,64]{1,0:T(1,128)} %bitcast.54), custom_call_target="tpu_custom_call" | custom-call | tf_op jit(solution)/shard_map/head/pallas_call | solution.py:109
  3.5 0.6 %collective-permute-start.1 = (f32[1,168,128]{2,1,0:T(8,128)S(1)}, f32[1,168,128]{2,1,0:T(8,128)S(1)}, u32[]{:S(2)}, u32[]{:S(2)}) collective-permute-start(f32[1,168,128]{2,1,0:T(8,128)S(1)} %get-tuple-element.19), channel_id=1, source_target_pairs={{0,1},{1,0},{2,3},{3,2},{4,5},{5,4},{6,7},{7,6},{8,9},{9,8},{10,11... | collective-permute-start | bytes 258056 | tf_op jit(solution)/shard_map/ppermute | solution.py:197
  4.1 0.1 collective-permute-start
  4.1 0.8 %collective-permute-done.1 = f32[1,168,128]{2,1,0:T(8,128)S(1)} collective-permute-done((f32[1,168,128]{2,1,0:T(8,128)S(1)}, f32[1,168,128]{2,1,0:T(8,128)S(1)}, u32[]{:S(2)}, u32[]{:S(2)}) %collective-permute-start.1) | collective-permute-done | bytes 86048 | tf_op jit(solution)/shard_map/ppermute | solution.py:197
  5.0 2.9 %collective-permute-start.2 = (f32[168,128]{1,0:T(8,128)S(1)}, f32[168,128]{1,0:T(8,128)S(1)}, u32[]{:S(2)}, u32[]{:S(2)}) collective-permute-start(f32[168,128]{1,0:T(8,128)S(1)} %bitcast_add_fusion.3), channel_id=1, source_target_pairs={{0,2},{2,0},{4,6},{6,4},{1,3},{3,1},{5,7},{7,5},{8,10},{10,8},{12,... | collective-permute-start | bytes 258056 | tf_op jit(solution)/shard_map/ppermute | solution.py:197
  7.9 0.0 collective-permute-done
  7.9 1.6 %collective-permute-start.4 = (f32[168,128]{1,0:T(8,128)S(1)}, f32[168,128]{1,0:T(8,128)S(1)}, u32[]{:S(2)}, u32[]{:S(2)}) collective-permute-start(f32[168,128]{1,0:T(8,128)S(1)} %get-tuple-element.16), channel_id=1, source_target_pairs={{0,6},{2,4},{4,2},{6,0},{1,7},{3,5},{5,3},{7,1},{8,14},{10,12},{12... | collective-permute-start | bytes 258056 | tf_op jit(solution)/shard_map/ppermute | solution.py:197
  9.5 0.4 collective-permute-start.3
  9.8 0.9 %collective-permute-done.2 = f32[168,128]{1,0:T(8,128)S(1)} collective-permute-done((f32[168,128]{1,0:T(8,128)S(1)}, f32[168,128]{1,0:T(8,128)S(1)}, u32[]{:S(2)}, u32[]{:S(2)}) %collective-permute-start.2) | collective-permute-done | bytes 86048 | tf_op jit(solution)/shard_map/ppermute | solution.py:197
  10.7 3.1 %collective-permute-done.4 = f32[168,128]{1,0:T(8,128)S(1)} collective-permute-done((f32[168,128]{1,0:T(8,128)S(1)}, f32[168,128]{1,0:T(8,128)S(1)}, u32[]{:S(2)}, u32[]{:S(2)}) %collective-permute-start.4) | collective-permute-done | bytes 86048 | tf_op jit(solution)/shard_map/ppermute | solution.py:197
  13.9 1.5 %collective-permute-done.3 = f32[168,128]{1,0:T(8,128)S(1)} collective-permute-done((f32[168,128]{1,0:T(8,128)S(1)}, f32[168,128]{1,0:T(8,128)S(1)}, u32[]{:S(2)}, u32[]{:S(2)}) %collective-permute-start.3) | collective-permute-done | bytes 86048 | tf_op jit(solution)/shard_map/ppermute | solution.py:197
  15.4 3.7 %collective-permute-start.7 = (f32[168,128]{1,0:T(8,128)S(1)}, f32[168,128]{1,0:T(8,128)S(1)}, u32[]{:S(2)}, u32[]{:S(2)}) collective-permute-start(f32[168,128]{1,0:T(8,128)S(1)} %fusion.1), channel_id=1, source_target_pairs={{0,24},{8,16},{16,8},{24,0},{1,25},{9,17},{17,9},{25,1},{2,26},{10... | collective-permute-start | bytes 258056 | tf_op jit(solution)/shard_map/ppermute | solution.py:197
  19.1 0.0 collective-permute-start.6
  19.1 0.8 %collective-permute-start.5 = (f32[168,128]{1,0:T(8,128)S(1)}, f32[168,128]{1,0:T(8,128)S(1)}, u32[]{:S(2)}, u32[]{:S(2)}) collective-permute-start(f32[168,128]{1,0:T(8,128)S(1)} %fusion.1), channel_id=1, source_target_pairs={{0,8},{8,0},{16,24},{24,16},{1,9},{9,1},{17,25},{25,17},{2,10},{10... | collective-permute-start | bytes 258056 | tf_op jit(solution)/shard_map/ppermute | solution.py:197
  19.8 2.6 %collective-permute-done.7 = f32[168,128]{1,0:T(8,128)S(1)} collective-permute-done((f32[168,128]{1,0:T(8,128)S(1)}, f32[168,128]{1,0:T(8,128)S(1)}, u32[]{:S(2)}, u32[]{:S(2)}) %collective-permute-start.7) | collective-permute-done | bytes 86048 | tf_op jit(solution)/shard_map/ppermute | solution.py:197
  22.5 3.7 %collective-permute-done.6 = f32[168,128]{1,0:T(8,128)S(1)} collective-permute-done((f32[168,128]{1,0:T(8,128)S(1)}, f32[168,128]{1,0:T(8,128)S(1)}, u32[]{:S(2)}, u32[]{:S(2)}) %collective-permute-start.6) | collective-permute-done | bytes 86048 | tf_op jit(solution)/shard_map/ppermute | solution.py:197
  26.2 0.0 collective-permute-done.5
  26.3 0.8 %collective-permute-start.11 = (f32[168,128]{1,0:T(8,128)S(1)}, f32[168,128]{1,0:T(8,128)S(1)}, u32[]{:S(2)}, u32[]{:S(2)}) collective-permute-start(f32[168,128]{1,0:T(8,128)S(1)} %get-tuple-element.15), channel_id=1, source_target_pairs={{0,4},{2,6},{4,0},{6,2},{1,5},{3,7},{5,1},{7,3},{8,12},{10,14},{12... | collective-permute-start | bytes 258056 | tf_op jit(solution)/shard_map/ppermute | solution.py:197
  27.1 1.2 %collective-permute-start.9 = (f32[168,128]{1,0:T(8,128)S(1)}, f32[168,128]{1,0:T(8,128)S(1)}, u32[]{:S(2)}, u32[]{:S(2)}) collective-permute-start(f32[168,128]{1,0:T(8,128)S(1)} %get-tuple-element.15), channel_id=1, source_target_pairs={{0,2},{2,0},{4,6},{6,4},{1,3},{3,1},{5,7},{7,5},{8,10},{10,8},{12,... | collective-permute-start | bytes 258056 | tf_op jit(solution)/shard_map/ppermute | solution.py:197
  28.3 0.0 collective-permute-start.8
  28.3 1.5 %collective-permute-start.13 = (f32[168,128]{1,0:T(8,128)S(1)}, f32[168,128]{1,0:T(8,128)S(1)}, u32[]{:S(2)}, u32[]{:S(2)}) collective-permute-start(f32[168,128]{1,0:T(8,128)S(1)} %get-tuple-element.15), channel_id=1, source_target_pairs={{0,6},{2,4},{4,2},{6,0},{1,7},{3,5},{5,3},{7,1},{8,14},{10,12},{12... | collective-permute-start | bytes 258056 | tf_op jit(solution)/shard_map/ppermute | solution.py:197
  29.8 1.0 %collective-permute-done.11 = f32[168,128]{1,0:T(8,128)S(1)} collective-permute-done((f32[168,128]{1,0:T(8,128)S(1)}, f32[168,128]{1,0:T(8,128)S(1)}, u32[]{:S(2)}, u32[]{:S(2)}) %collective-permute-start.11) | collective-permute-done | bytes 86048 | tf_op jit(solution)/shard_map/ppermute | solution.py:197
  30.8 0.0 collective-permute-start.12
  30.8 0.7 %collective-permute-done.9 = f32[168,128]{1,0:T(8,128)S(1)} collective-permute-done((f32[168,128]{1,0:T(8,128)S(1)}, f32[168,128]{1,0:T(8,128)S(1)}, u32[]{:S(2)}, u32[]{:S(2)}) %collective-permute-start.9) | collective-permute-done | bytes 86048 | tf_op jit(solution)/shard_map/ppermute | solution.py:197
  31.6 0.0 collective-permute-start.10
  31.6 0.0 collective-permute-done.8
  31.6 2.5 %collective-permute-done.13 = f32[168,128]{1,0:T(8,128)S(1)} collective-permute-done((f32[168,128]{1,0:T(8,128)S(1)}, f32[168,128]{1,0:T(8,128)S(1)}, u32[]{:S(2)}, u32[]{:S(2)}) %collective-permute-start.13) | collective-permute-done | bytes 86048 | tf_op jit(solution)/shard_map/ppermute | solution.py:197
  34.1 0.0 collective-permute-start.14
  34.1 0.0 collective-permute-done.10
  34.2 0.0 collective-permute-done.12
  34.2 1.2 %collective-permute-done.14 = f32[168,128]{1,0:T(8,128)S(1)} collective-permute-done((f32[168,128]{1,0:T(8,128)S(1)}, f32[168,128]{1,0:T(8,128)S(1)}, u32[]{:S(2)}, u32[]{:S(2)}) %collective-permute-start.14) | collective-permute-done | bytes 86048 | tf_op jit(solution)/shard_map/ppermute | solution.py:231
  35.4 1.3 %tail.1 = (f32[512,512]{1,0:T(8,128)}, f32[64,512]{1,0:T(8,128)}, f32[64,512]{1,0:T(8,128)}, f32[64,512]{1,0:T(8,128)}) custom-call(f32[1344,128]{1,0:T(8,128)S(1)} %bitcast.48, f32[64,512]{1,0:T(8,128)S(1)} %get-tuple-element.11.modes_ref, bf16[128,512]{1,0:T(8,128)(2,1)S(1)} %get-tuple-element.12.e_ref, f32[64,128]{1,0:T(8,128)S(1)} %get-tuple-element.13.scale_ref), custom_call_target="tpu_custom_call" | custom-call | tf_op jit(solution)/shard_map/tail/pallas_call | solution.py:171
  (14 shorter events, 0.3 us)
Async XLA Ops:
  3.5 1.5 %collective-permute-start.1 = (f32[1,168,128]{2,1,0:T(8,128)S(1)}, f32[1,168,128]{2,1,0:T(8,128)S(1)}, u32[]{:S(2)}, u32[]{:S(2)}) collective-permute-start(f32[1,168,128]{2,1,0:T(8,128)S(1)} %get-tuple-element.19), channel_id=1, source_target_pairs={{0,1},{1,0},{2,3},{3,2},{4,5},{5,4},{6,7},{7,6},{8,9},{9,8},{10,11... | collective-permute-start | bytes 258056 | tf_op jit(solution)/shard_map/ppermute | solution.py:197
  4.1 3.8 %collective-permute-start = (f32[3,168,128]{2,1,0:T(8,128)S(1)}, f32[3,168,128]{2,1,0:T(8,128)S(1)}, u32[]{:S(2)}, u32[]{:S(2)}) collective-permute-start(f32[3,168,128]{2,1,0:T(8,128)S(1)} %pad_maximum_fusion), channel_id=1, source_target_pairs={{0,1},{1,0},{2,3},{3,2},{4,5},{5,4},{6,7},{7,6},{8,9},{9,8},{10,11... | collective-permute-start | bytes 774152 | tf_op jit(solution)/shard_map/ppermute | solution.py:197
  5.0 5.7 %collective-permute-start.2 = (f32[168,128]{1,0:T(8,128)S(1)}, f32[168,128]{1,0:T(8,128)S(1)}, u32[]{:S(2)}, u32[]{:S(2)}) collective-permute-start(f32[168,128]{1,0:T(8,128)S(1)} %bitcast_add_fusion.3), channel_id=1, source_target_pairs={{0,2},{2,0},{4,6},{6,4},{1,3},{3,1},{5,7},{7,5},{8,10},{10,8},{12,... | collective-permute-start | bytes 258056 | tf_op jit(solution)/shard_map/ppermute | solution.py:197
  7.9 6.0 %collective-permute-start.4 = (f32[168,128]{1,0:T(8,128)S(1)}, f32[168,128]{1,0:T(8,128)S(1)}, u32[]{:S(2)}, u32[]{:S(2)}) collective-permute-start(f32[168,128]{1,0:T(8,128)S(1)} %get-tuple-element.16), channel_id=1, source_target_pairs={{0,6},{2,4},{4,2},{6,0},{1,7},{3,5},{5,3},{7,1},{8,14},{10,12},{12... | collective-permute-start | bytes 258056 | tf_op jit(solution)/shard_map/ppermute | solution.py:197
  9.5 5.9 %collective-permute-start.3 = (f32[168,128]{1,0:T(8,128)S(1)}, f32[168,128]{1,0:T(8,128)S(1)}, u32[]{:S(2)}, u32[]{:S(2)}) collective-permute-start(f32[168,128]{1,0:T(8,128)S(1)} %get-tuple-element.17), channel_id=1, source_target_pairs={{0,4},{2,6},{4,0},{6,2},{1,5},{3,7},{5,1},{7,3},{8,12},{10,14},{12... | collective-permute-start | bytes 258056 | tf_op jit(solution)/shard_map/ppermute | solution.py:197
  15.4 7.1 %collective-permute-start.7 = (f32[168,128]{1,0:T(8,128)S(1)}, f32[168,128]{1,0:T(8,128)S(1)}, u32[]{:S(2)}, u32[]{:S(2)}) collective-permute-start(f32[168,128]{1,0:T(8,128)S(1)} %fusion.1), channel_id=1, source_target_pairs={{0,24},{8,16},{16,8},{24,0},{1,25},{9,17},{17,9},{25,1},{2,26},{10... | collective-permute-start | bytes 258056 | tf_op jit(solution)/shard_map/ppermute | solution.py:197
  19.1 7.1 %collective-permute-start.6 = (f32[168,128]{1,0:T(8,128)S(1)}, f32[168,128]{1,0:T(8,128)S(1)}, u32[]{:S(2)}, u32[]{:S(2)}) collective-permute-start(f32[168,128]{1,0:T(8,128)S(1)} %fusion.1), channel_id=1, source_target_pairs={{0,16},{8,24},{16,0},{24,8},{1,17},{9,25},{17,1},{25,9},{2,18},{10... | collective-permute-start | bytes 258056 | tf_op jit(solution)/shard_map/ppermute | solution.py:197
  19.1 7.1 %collective-permute-start.5 = (f32[168,128]{1,0:T(8,128)S(1)}, f32[168,128]{1,0:T(8,128)S(1)}, u32[]{:S(2)}, u32[]{:S(2)}) collective-permute-start(f32[168,128]{1,0:T(8,128)S(1)} %fusion.1), channel_id=1, source_target_pairs={{0,8},{8,0},{16,24},{24,16},{1,9},{9,1},{17,25},{25,17},{2,10},{10... | collective-permute-start | bytes 258056 | tf_op jit(solution)/shard_map/ppermute | solution.py:197
  26.3 4.6 %collective-permute-start.11 = (f32[168,128]{1,0:T(8,128)S(1)}, f32[168,128]{1,0:T(8,128)S(1)}, u32[]{:S(2)}, u32[]{:S(2)}) collective-permute-start(f32[168,128]{1,0:T(8,128)S(1)} %get-tuple-element.15), channel_id=1, source_target_pairs={{0,4},{2,6},{4,0},{6,2},{1,5},{3,7},{5,1},{7,3},{8,12},{10,14},{12... | collective-permute-start | bytes 258056 | tf_op jit(solution)/shard_map/ppermute | solution.py:197
  27.1 4.5 %collective-permute-start.9 = (f32[168,128]{1,0:T(8,128)S(1)}, f32[168,128]{1,0:T(8,128)S(1)}, u32[]{:S(2)}, u32[]{:S(2)}) collective-permute-start(f32[168,128]{1,0:T(8,128)S(1)} %get-tuple-element.15), channel_id=1, source_target_pairs={{0,2},{2,0},{4,6},{6,4},{1,3},{3,1},{5,7},{7,5},{8,10},{10,8},{12,... | collective-permute-start | bytes 258056 | tf_op jit(solution)/shard_map/ppermute | solution.py:197
  28.3 3.3 %collective-permute-start.8 = (f32[168,128]{1,0:T(8,128)S(1)}, f32[168,128]{1,0:T(8,128)S(1)}, u32[]{:S(2)}, u32[]{:S(2)}) collective-permute-start(f32[168,128]{1,0:T(8,128)S(1)} %get-tuple-element.15), channel_id=1, source_target_pairs={{0,1},{1,0},{2,3},{3,2},{4,5},{5,4},{6,7},{7,6},{8,9},{9,8},{10,11... | collective-permute-start | bytes 258056 | tf_op jit(solution)/shard_map/ppermute | solution.py:231
  28.3 5.8 %collective-permute-start.13 = (f32[168,128]{1,0:T(8,128)S(1)}, f32[168,128]{1,0:T(8,128)S(1)}, u32[]{:S(2)}, u32[]{:S(2)}) collective-permute-start(f32[168,128]{1,0:T(8,128)S(1)} %get-tuple-element.15), channel_id=1, source_target_pairs={{0,6},{2,4},{4,2},{6,0},{1,7},{3,5},{5,3},{7,1},{8,14},{10,12},{12... | collective-permute-start | bytes 258056 | tf_op jit(solution)/shard_map/ppermute | solution.py:197
  30.8 3.4 %collective-permute-start.12 = (f32[168,128]{1,0:T(8,128)S(1)}, f32[168,128]{1,0:T(8,128)S(1)}, u32[]{:S(2)}, u32[]{:S(2)}) collective-permute-start(f32[168,128]{1,0:T(8,128)S(1)} %collective-permute-done.11), channel_id=1, source_target_pairs={{0,1},{1,0},{2,3},{3,2},{4,5},{5,4},{6,7},{7,6},{8,9},{9,8},{10,11... | collective-permute-start | bytes 258056 | tf_op jit(solution)/shard_map/ppermute | solution.py:231
  31.6 2.6 %collective-permute-start.10 = (f32[168,128]{1,0:T(8,128)S(1)}, f32[168,128]{1,0:T(8,128)S(1)}, u32[]{:S(2)}, u32[]{:S(2)}) collective-permute-start(f32[168,128]{1,0:T(8,128)S(1)} %collective-permute-done.9), channel_id=1, source_target_pairs={{0,1},{1,0},{2,3},{3,2},{4,5},{5,4},{6,7},{7,6},{8,9},{9,8},{10,11... | collective-permute-start | bytes 258056 | tf_op jit(solution)/shard_map/ppermute | solution.py:231
  34.1 1.3 %collective-permute-start.14 = (f32[168,128]{1,0:T(8,128)S(1)}, f32[168,128]{1,0:T(8,128)S(1)}, u32[]{:S(2)}, u32[]{:S(2)}) collective-permute-start(f32[168,128]{1,0:T(8,128)S(1)} %collective-permute-done.13), channel_id=1, source_target_pairs={{0,1},{1,0},{2,3},{3,2},{4,5},{5,4},{6,7},{7,6},{8,9},{9,8},{10,11... | collective-permute-start | bytes 258056 | tf_op jit(solution)/shard_map/ppermute | solution.py:231

commit v5 on v4

--- a/solution.py
+++ b/solution.py
@@ -124,7 +124,7 @@
 
 
 def tail_kernel(
-    packed_ref, modes_ref, e_ref, scale_ref, gram_hbm, modes_hbm, train_hbm, valid_hbm, gram, train_ref, sems
+    packed_ref, e_ref, scale_ref, gram_hbm, train_hbm, valid_hbm, gram, train_ref, sems
 ):
     m, k = train_ref.shape
     half = k // 2
@@ -153,7 +153,6 @@
     gram[half:, :half] = b.T
     send(gram.at[second, first], gram_hbm.at[second, first])
     gram[:half, half:] = b
-    send(modes_ref, modes_hbm)
     for j in range(k // LANES):
         send(packed_ref.at[pl.ds(valid + j * m, m)], valid_hbm.at[:, pl.ds(j * LANES, LANES)])
     g_high, g_low = split(gram[...])
@@ -164,19 +163,19 @@
         copy.wait()
 
 
-def tail(packed, modes, e_both, scales):
+def tail(packed, e_both, scales):
     m, k = scales.shape[0], e_both.shape[1]
     hbm, vmem = pl.BlockSpec(memory_space=pltpu.HBM), pl.BlockSpec(memory_space=pltpu.VMEM)
     coef = pltpu.HBM((m, k), F32)
     return pl.pallas_call(
         tail_kernel,
-        out_shape=(pltpu.HBM((k, k), F32), pltpu.HBM(modes.shape, F32), coef, coef),
-        in_specs=[vmem] * 4,
-        out_specs=(hbm,) * 4,
-        scratch_shapes=[pltpu.VMEM((k, k), F32), pltpu.VMEM((m, k), F32), pltpu.SemaphoreType.DMA((3 * k // (2 * LANES) + 5,))],
+        out_shape=(pltpu.HBM((k, k), F32), coef, coef),
+        in_specs=[vmem] * 3,
+        out_specs=(hbm,) * 3,
+        scratch_shapes=[pltpu.VMEM((k, k), F32), pltpu.VMEM((m, k), F32), pltpu.SemaphoreType.DMA((3 * k // (2 * LANES) + 4,))],
         compiler_params=pltpu.CompilerParams(vmem_limit_bytes=16 * 1024 * 1024),
         name="tail",
-    )(packed, modes, e_both, scales)
+    )(packed, e_both, scales)
 
 
 def partners(n, r):
@@ -245,7 +244,8 @@
     own = reduce_scatter(packed.reshape(cores, chips, piece, LANES))
     own = all_reduce(own, "plane")
     packed = all_gather(own, "core", "chip").reshape(-1, LANES)
-    return tail(packed, modes, e_both, scales)
+    gram, train_coef, valid_coef = tail(packed, e_both, scales)
+    return gram, modes, train_coef, valid_coef
 
 
 def solution(mesh):

time: 36.9 us -> 36.4 us (0.986)
  waiting for transfers between devices: 18.2 us -> 17 us
  local copies, waits for them, and re-layouts: 0.18 us -> 0.83 us
    ppermute x11, waiting for transfers between devices: 17 us -> 15.8 us  [permute(): return lax.ppermute(x, axis, partners(lax.axis_size(axis), r))]
    unnamed x0 -> x1, local copies, waits for them, and re-layouts: none -> 0.66 us
  transfers between devices with their start and end apart: 15 -> 15, of which waited for: 10 -> 11; matrix products, arithmetic and copies ran while one was open for 0% -> 2% of each run, Pallas kernels for 0% -> 0%
where the time goes in v5:
time: 36.4 us; the launch traced here: 36.2 us
  waiting for transfers between devices  17 us (47%)
  starting transfers between devices  13.5 us (37%)
  Pallas kernels  4.03 us (11%)
  local copies, waits for them, and re-layouts  0.83 us (2%)
  between operations  0.75 us (2%)
    ppermute x11, waiting for transfers between devices, permute(): return lax.ppermute(x, axis, partners(lax.axis_size(axis), r))  15.8 us
    ppermute x11, starting transfers between devices, permute(): return lax.ppermute(x, axis, partners(lax.axis_size(axis), r))  13.5 us
    pallas_call x1, Pallas kernels, head(): pl.pallas_call(functools.partial(head_kernel, total), out_shape=(pltpu.VM...  2.77 us
    pallas_call x1, Pallas kernels, tail(): pl.pallas_call(tail_kernel, out_shape=(pltpu.HBM((k, k), F32), coef, coef...  1.27 us
    ppermute x4, waiting for transfers between devices, all_gather(): there = row if q == 0 else lax.ppermute(row, outer, partners(no, q))  1.19 us
  transfers between devices with their start and end apart: 15, of which 11 were waited for; matrix products, arithmetic and copies ran while one was open for 2% of the time, Pallas kernels for 0%

profile of v5, /device:TPU:0, one launch (start us, length us, event | category | flops | bytes accessed | tf_op | source)
XLA Modules:
  0.0 36.2 jit_solution(1991777535872180093)
XLA Ops:
  0.7 2.8 %head.1 = (f32[1344,128]{1,0:T(8,128)S(1)}, f32[64,512]{1,0:T(8,128)S(1)}, bf16[128,512]{1,0:T(8,128)(2,1)S(1)}, f32[64,128]{1,0:T(8,128)S(1)}) custom-call(f32[512,512]{1,0:T(8,128)} %s_hbm.1, f32[512,512]{1,0:T(8,128)} %v_hbm.1, f32[64,512]{1,0:T(8,128)} %bitcast.53, f32[1,64]{1,0:T(1,128)} %bitcast.54), custom_call_target="tpu_custom_call" | custom-call | tf_op jit(solution)/shard_map/head/pallas_call | solution.py:109
  3.5 0.6 %collective-permute-start.1 = (f32[1,168,128]{2,1,0:T(8,128)S(1)}, f32[1,168,128]{2,1,0:T(8,128)S(1)}, u32[]{:S(2)}, u32[]{:S(2)}) collective-permute-start(f32[1,168,128]{2,1,0:T(8,128)S(1)} %get-tuple-element.25), channel_id=1, source_target_pairs={{0,1},{1,0},{2,3},{3,2},{4,5},{5,4},{6,7},{7,6},{8,9},{9,8},{10,11... | collective-permute-start | bytes 258056 | tf_op jit(solution)/shard_map/ppermute | solution.py:196
  4.1 0.1 collective-permute-start
  4.1 0.8 %collective-permute-done.1 = f32[1,168,128]{2,1,0:T(8,128)S(1)} collective-permute-done((f32[1,168,128]{2,1,0:T(8,128)S(1)}, f32[1,168,128]{2,1,0:T(8,128)S(1)}, u32[]{:S(2)}, u32[]{:S(2)}) %collective-permute-start.1) | collective-permute-done | bytes 86048 | tf_op jit(solution)/shard_map/ppermute | solution.py:196
  5.0 2.9 %collective-permute-start.2 = (f32[168,128]{1,0:T(8,128)S(1)}, f32[168,128]{1,0:T(8,128)S(1)}, u32[]{:S(2)}, u32[]{:S(2)}) collective-permute-start(f32[168,128]{1,0:T(8,128)S(1)} %bitcast_add_fusion.3), channel_id=1, source_target_pairs={{0,2},{2,0},{4,6},{6,4},{1,3},{3,1},{5,7},{7,5},{8,10},{10,8},{12,... | collective-permute-start | bytes 258056 | tf_op jit(solution)/shard_map/ppermute | solution.py:196
  7.9 0.0 collective-permute-done
  7.9 1.6 %collective-permute-start.3 = (f32[168,128]{1,0:T(8,128)S(1)}, f32[168,128]{1,0:T(8,128)S(1)}, u32[]{:S(2)}, u32[]{:S(2)}) collective-permute-start(f32[168,128]{1,0:T(8,128)S(1)} %get-tuple-element.23), channel_id=1, source_target_pairs={{0,4},{2,6},{4,0},{6,2},{1,5},{3,7},{5,1},{7,3},{8,12},{10,14},{12... | collective-permute-start | bytes 258056 | tf_op jit(solution)/shard_map/ppermute | solution.py:196
  9.5 0.3 collective-permute-start.4
  9.8 0.9 %collective-permute-done.2 = f32[168,128]{1,0:T(8,128)S(1)} collective-permute-done((f32[168,128]{1,0:T(8,128)S(1)}, f32[168,128]{1,0:T(8,128)S(1)}, u32[]{:S(2)}, u32[]{:S(2)}) %collective-permute-start.2) | collective-permute-done | bytes 86048 | tf_op jit(solution)/shard_map/ppermute | solution.py:196
  10.7 2.6 %collective-permute-done.3 = f32[168,128]{1,0:T(8,128)S(1)} collective-permute-done((f32[168,128]{1,0:T(8,128)S(1)}, f32[168,128]{1,0:T(8,128)S(1)}, u32[]{:S(2)}, u32[]{:S(2)}) %collective-permute-start.3) | collective-permute-done | bytes 86048 | tf_op jit(solution)/shard_map/ppermute | solution.py:196
  13.4 1.5 %collective-permute-done.4 = f32[168,128]{1,0:T(8,128)S(1)} collective-permute-done((f32[168,128]{1,0:T(8,128)S(1)}, f32[168,128]{1,0:T(8,128)S(1)}, u32[]{:S(2)}, u32[]{:S(2)}) %collective-permute-start.4) | collective-permute-done | bytes 86048 | tf_op jit(solution)/shard_map/ppermute | solution.py:196
  14.9 1.6 %collective-permute-start.5 = (f32[168,128]{1,0:T(8,128)S(1)}, f32[168,128]{1,0:T(8,128)S(1)}, u32[]{:S(2)}, u32[]{:S(2)}) collective-permute-start(f32[168,128]{1,0:T(8,128)S(1)} %fusion.1), channel_id=1, source_target_pairs={{0,8},{8,0},{16,24},{24,16},{1,9},{9,1},{17,25},{25,17},{2,10},{10... | collective-permute-start | bytes 258056 | tf_op jit(solution)/shard_map/ppermute | solution.py:196
  16.5 2.6 %collective-permute-start.6 = (f32[168,128]{1,0:T(8,128)S(1)}, f32[168,128]{1,0:T(8,128)S(1)}, u32[]{:S(2)}, u32[]{:S(2)}) collective-permute-start(f32[168,128]{1,0:T(8,128)S(1)} %fusion.1), channel_id=1, source_target_pairs={{0,16},{8,24},{16,0},{24,8},{1,17},{9,25},{17,1},{25,9},{2,18},{10... | collective-permute-start | bytes 258056 | tf_op jit(solution)/shard_map/ppermute | solution.py:196
  19.1 0.2 collective-permute-start.7
  19.4 0.6 %collective-permute-done.5 = f32[168,128]{1,0:T(8,128)S(1)} collective-permute-done((f32[168,128]{1,0:T(8,128)S(1)}, f32[168,128]{1,0:T(8,128)S(1)}, u32[]{:S(2)}, u32[]{:S(2)}) %collective-permute-start.5) | collective-permute-done | bytes 86048 | tf_op jit(solution)/shard_map/ppermute | solution.py:196
  20.0 3.8 %collective-permute-done.6 = f32[168,128]{1,0:T(8,128)S(1)} collective-permute-done((f32[168,128]{1,0:T(8,128)S(1)}, f32[168,128]{1,0:T(8,128)S(1)}, u32[]{:S(2)}, u32[]{:S(2)}) %collective-permute-start.6) | collective-permute-done | bytes 86048 | tf_op jit(solution)/shard_map/ppermute | solution.py:196
  23.8 1.7 %collective-permute-done.7 = f32[168,128]{1,0:T(8,128)S(1)} collective-permute-done((f32[168,128]{1,0:T(8,128)S(1)}, f32[168,128]{1,0:T(8,128)S(1)}, u32[]{:S(2)}, u32[]{:S(2)}) %collective-permute-start.7) | collective-permute-done | bytes 86048 | tf_op jit(solution)/shard_map/ppermute | solution.py:196
  25.6 0.6 %collective-permute-start.9 = (f32[168,128]{1,0:T(8,128)S(1)}, f32[168,128]{1,0:T(8,128)S(1)}, u32[]{:S(2)}, u32[]{:S(2)}) collective-permute-start(f32[168,128]{1,0:T(8,128)S(1)} %get-tuple-element.21), channel_id=1, source_target_pairs={{0,2},{2,0},{4,6},{6,4},{1,3},{3,1},{5,7},{7,5},{8,10},{10,8},{12,... | collective-permute-start | bytes 258056 | tf_op jit(solution)/shard_map/ppermute | solution.py:196
  26.2 0.0 collective-permute-start.8
  26.2 0.7 %copy.16 = f32[64,512]{1,0:T(8,128)} copy(f32[64,512]{1,0:T(8,128)S(1)} %get-tuple-element.29) | data formatting | bytes 262144
  26.9 1.1 %collective-permute-start.11 = (f32[168,128]{1,0:T(8,128)S(1)}, f32[168,128]{1,0:T(8,128)S(1)}, u32[]{:S(2)}, u32[]{:S(2)}) collective-permute-start(f32[168,128]{1,0:T(8,128)S(1)} %get-tuple-element.21), channel_id=1, source_target_pairs={{0,4},{2,6},{4,0},{6,2},{1,5},{3,7},{5,1},{7,3},{8,12},{10,14},{12... | collective-permute-start | bytes 258056 | tf_op jit(solution)/shard_map/ppermute | solution.py:196
  28.0 1.8 %collective-permute-start.13 = (f32[168,128]{1,0:T(8,128)S(1)}, f32[168,128]{1,0:T(8,128)S(1)}, u32[]{:S(2)}, u32[]{:S(2)}) collective-permute-start(f32[168,128]{1,0:T(8,128)S(1)} %get-tuple-element.21), channel_id=1, source_target_pairs={{0,6},{2,4},{4,2},{6,0},{1,7},{3,5},{5,3},{7,1},{8,14},{10,12},{12... | collective-permute-start | bytes 258056 | tf_op jit(solution)/shard_map/ppermute | solution.py:196
  29.8 0.3 collective-permute-done.9
  30.1 0.0 collective-permute-start.10
  30.2 0.0 collective-permute-done.8
  30.2 2.1 %collective-permute-done.11 = f32[168,128]{1,0:T(8,128)S(1)} collective-permute-done((f32[168,128]{1,0:T(8,128)S(1)}, f32[168,128]{1,0:T(8,128)S(1)}, u32[]{:S(2)}, u32[]{:S(2)}) %collective-permute-start.11) | collective-permute-done | bytes 86048 | tf_op jit(solution)/shard_map/ppermute | solution.py:196
  32.3 0.0 collective-permute-start.12
  32.3 1.3 %collective-permute-done.13 = f32[168,128]{1,0:T(8,128)S(1)} collective-permute-done((f32[168,128]{1,0:T(8,128)S(1)}, f32[168,128]{1,0:T(8,128)S(1)}, u32[]{:S(2)}, u32[]{:S(2)}) %collective-permute-start.13) | collective-permute-done | bytes 86048 | tf_op jit(solution)/shard_map/ppermute | solution.py:196
  33.6 0.0 collective-permute-start.14
  33.7 0.0 collective-permute-done.12
  33.8 1.2 %collective-permute-done.14 = f32[168,128]{1,0:T(8,128)S(1)} collective-permute-done((f32[168,128]{1,0:T(8,128)S(1)}, f32[168,128]{1,0:T(8,128)S(1)}, u32[]{:S(2)}, u32[]{:S(2)}) %collective-permute-start.14) | collective-permute-done | bytes 86048 | tf_op jit(solution)/shard_map/ppermute | solution.py:230
  34.9 1.3 %tail.1 = (f32[512,512]{1,0:T(8,128)}, f32[64,512]{1,0:T(8,128)}, f32[64,512]{1,0:T(8,128)}) custom-call(f32[1344,128]{1,0:T(8,128)S(1)} %bitcast.48, bf16[128,512]{1,0:T(8,128)(2,1)S(1)} %get-tuple-element.14.e_ref, f32[64,128]{1,0:T(8,128)S(1)} %get-tuple-element.15.scale_ref), custom_call_target="tpu_custom_call" | custom-call | tf_op jit(solution)/shard_map/tail/pallas_call | solution.py:170
  (15 shorter events, 0.3 us)
Async XLA Ops:
  3.5 1.5 %collective-permute-start.1 = (f32[1,168,128]{2,1,0:T(8,128)S(1)}, f32[1,168,128]{2,1,0:T(8,128)S(1)}, u32[]{:S(2)}, u32[]{:S(2)}) collective-permute-start(f32[1,168,128]{2,1,0:T(8,128)S(1)} %get-tuple-element.25), channel_id=1, source_target_pairs={{0,1},{1,0},{2,3},{3,2},{4,5},{5,4},{6,7},{7,6},{8,9},{9,8},{10,11... | collective-permute-start | bytes 258056 | tf_op jit(solution)/shard_map/ppermute | solution.py:196
  4.1 3.8 %collective-permute-start = (f32[3,168,128]{2,1,0:T(8,128)S(1)}, f32[3,168,128]{2,1,0:T(8,128)S(1)}, u32[]{:S(2)}, u32[]{:S(2)}) collective-permute-start(f32[3,168,128]{2,1,0:T(8,128)S(1)} %pad_maximum_fusion), channel_id=1, source_target_pairs={{0,1},{1,0},{2,3},{3,2},{4,5},{5,4},{6,7},{7,6},{8,9},{9,8},{10,11... | collective-permute-start | bytes 774152 | tf_op jit(solution)/shard_map/ppermute | solution.py:196
  5.0 5.7 %collective-permute-start.2 = (f32[168,128]{1,0:T(8,128)S(1)}, f32[168,128]{1,0:T(8,128)S(1)}, u32[]{:S(2)}, u32[]{:S(2)}) collective-permute-start(f32[168,128]{1,0:T(8,128)S(1)} %bitcast_add_fusion.3), channel_id=1, source_target_pairs={{0,2},{2,0},{4,6},{6,4},{1,3},{3,1},{5,7},{7,5},{8,10},{10,8},{12,... | collective-permute-start | bytes 258056 | tf_op jit(solution)/shard_map/ppermute | solution.py:196
  7.9 5.5 %collective-permute-start.3 = (f32[168,128]{1,0:T(8,128)S(1)}, f32[168,128]{1,0:T(8,128)S(1)}, u32[]{:S(2)}, u32[]{:S(2)}) collective-permute-start(f32[168,128]{1,0:T(8,128)S(1)} %get-tuple-element.23), channel_id=1, source_target_pairs={{0,4},{2,6},{4,0},{6,2},{1,5},{3,7},{5,1},{7,3},{8,12},{10,14},{12... | collective-permute-start | bytes 258056 | tf_op jit(solution)/shard_map/ppermute | solution.py:196
  9.5 5.4 %collective-permute-start.4 = (f32[168,128]{1,0:T(8,128)S(1)}, f32[168,128]{1,0:T(8,128)S(1)}, u32[]{:S(2)}, u32[]{:S(2)}) collective-permute-start(f32[168,128]{1,0:T(8,128)S(1)} %get-tuple-element.22), channel_id=1, source_target_pairs={{0,6},{2,4},{4,2},{6,0},{1,7},{3,5},{5,3},{7,1},{8,14},{10,12},{12... | collective-permute-start | bytes 258056 | tf_op jit(solution)/shard_map/ppermute | solution.py:196
  14.9 5.1 %collective-permute-start.5 = (f32[168,128]{1,0:T(8,128)S(1)}, f32[168,128]{1,0:T(8,128)S(1)}, u32[]{:S(2)}, u32[]{:S(2)}) collective-permute-start(f32[168,128]{1,0:T(8,128)S(1)} %fusion.1), channel_id=1, source_target_pairs={{0,8},{8,0},{16,24},{24,16},{1,9},{9,1},{17,25},{25,17},{2,10},{10... | collective-permute-start | bytes 258056 | tf_op jit(solution)/shard_map/ppermute | solution.py:196
  16.5 7.2 %collective-permute-start.6 = (f32[168,128]{1,0:T(8,128)S(1)}, f32[168,128]{1,0:T(8,128)S(1)}, u32[]{:S(2)}, u32[]{:S(2)}) collective-permute-start(f32[168,128]{1,0:T(8,128)S(1)} %fusion.1), channel_id=1, source_target_pairs={{0,16},{8,24},{16,0},{24,8},{1,17},{9,25},{17,1},{25,9},{2,18},{10... | collective-permute-start | bytes 258056 | tf_op jit(solution)/shard_map/ppermute | solution.py:196
  19.1 6.4 %collective-permute-start.7 = (f32[168,128]{1,0:T(8,128)S(1)}, f32[168,128]{1,0:T(8,128)S(1)}, u32[]{:S(2)}, u32[]{:S(2)}) collective-permute-start(f32[168,128]{1,0:T(8,128)S(1)} %fusion.1), channel_id=1, source_target_pairs={{0,24},{8,16},{16,8},{24,0},{1,25},{9,17},{17,9},{25,1},{2,26},{10... | collective-permute-start | bytes 258056 | tf_op jit(solution)/shard_map/ppermute | solution.py:196
  25.6 4.5 %collective-permute-start.9 = (f32[168,128]{1,0:T(8,128)S(1)}, f32[168,128]{1,0:T(8,128)S(1)}, u32[]{:S(2)}, u32[]{:S(2)}) collective-permute-start(f32[168,128]{1,0:T(8,128)S(1)} %get-tuple-element.21), channel_id=1, source_target_pairs={{0,2},{2,0},{4,6},{6,4},{1,3},{3,1},{5,7},{7,5},{8,10},{10,8},{12,... | collective-permute-start | bytes 258056 | tf_op jit(solution)/shard_map/ppermute | solution.py:196
  26.2 4.0 %collective-permute-start.8 = (f32[168,128]{1,0:T(8,128)S(1)}, f32[168,128]{1,0:T(8,128)S(1)}, u32[]{:S(2)}, u32[]{:S(2)}) collective-permute-start(f32[168,128]{1,0:T(8,128)S(1)} %get-tuple-element.21), channel_id=1, source_target_pairs={{0,1},{1,0},{2,3},{3,2},{4,5},{5,4},{6,7},{7,6},{8,9},{9,8},{10,11... | collective-permute-start | bytes 258056 | tf_op jit(solution)/shard_map/ppermute | solution.py:230
  26.9 5.5 %collective-permute-start.11 = (f32[168,128]{1,0:T(8,128)S(1)}, f32[168,128]{1,0:T(8,128)S(1)}, u32[]{:S(2)}, u32[]{:S(2)}) collective-permute-start(f32[168,128]{1,0:T(8,128)S(1)} %get-tuple-element.21), channel_id=1, source_target_pairs={{0,4},{2,6},{4,0},{6,2},{1,5},{3,7},{5,1},{7,3},{8,12},{10,14},{12... | collective-permute-start | bytes 258056 | tf_op jit(solution)/shard_map/ppermute | solution.py:196
  28.0 5.7 %collective-permute-start.13 = (f32[168,128]{1,0:T(8,128)S(1)}, f32[168,128]{1,0:T(8,128)S(1)}, u32[]{:S(2)}, u32[]{:S(2)}) collective-permute-start(f32[168,128]{1,0:T(8,128)S(1)} %get-tuple-element.21), channel_id=1, source_target_pairs={{0,6},{2,4},{4,2},{6,0},{1,7},{3,5},{5,3},{7,1},{8,14},{10,12},{12... | collective-permute-start | bytes 258056 | tf_op jit(solution)/shard_map/ppermute | solution.py:196
  30.1 3.5 %collective-permute-start.10 = (f32[168,128]{1,0:T(8,128)S(1)}, f32[168,128]{1,0:T(8,128)S(1)}, u32[]{:S(2)}, u32[]{:S(2)}) collective-permute-start(f32[168,128]{1,0:T(8,128)S(1)} %collective-permute-done.9), channel_id=1, source_target_pairs={{0,1},{1,0},{2,3},{3,2},{4,5},{5,4},{6,7},{7,6},{8,9},{9,8},{10,11... | collective-permute-start | bytes 258056 | tf_op jit(solution)/shard_map/ppermute | solution.py:230
  32.3 1.4 %collective-permute-start.12 = (f32[168,128]{1,0:T(8,128)S(1)}, f32[168,128]{1,0:T(8,128)S(1)}, u32[]{:S(2)}, u32[]{:S(2)}) collective-permute-start(f32[168,128]{1,0:T(8,128)S(1)} %collective-permute-done.11), channel_id=1, source_target_pairs={{0,1},{1,0},{2,3},{3,2},{4,5},{5,4},{6,7},{7,6},{8,9},{9,8},{10,11... | collective-permute-start | bytes 258056 | tf_op jit(solution)/shard_map/ppermute | solution.py:230
  33.6 1.3 %collective-permute-start.14 = (f32[168,128]{1,0:T(8,128)S(1)}, f32[168,128]{1,0:T(8,128)S(1)}, u32[]{:S(2)}, u32[]{:S(2)}) collective-permute-start(f32[168,128]{1,0:T(8,128)S(1)} %collective-permute-done.13), channel_id=1, source_target_pairs={{0,1},{1,0},{2,3},{3,2},{4,5},{5,4},{6,7},{7,6},{8,9},{9,8},{10,11... | collective-permute-start | bytes 258056 | tf_op jit(solution)/shard_map/ppermute | solution.py:230

commit v6 on v4

--- a/solution.py
+++ b/solution.py
@@ -11,6 +11,8 @@
 LANES = 128
 DIRECT = 4
 F32 = jnp.float32
+SCATTER = ((1, 1), (2, 2), (3, 3))
+SPREAD = ((3, 3), (2, 1), (1, 2))
 
 
 def axes_of(mesh):
@@ -197,19 +199,33 @@
     return lax.ppermute(x, axis, partners(lax.axis_size(axis), r))
 
 
+def planar(cores, chips):
+    return cores == 2 and chips == DIRECT
+
+
+def reach(steps, core, i):
+    return jnp.where(core == 0, steps[i][0], steps[i][1]) if i < len(steps) else 0
+
+
+def swap(x, steps, i):
+    pairs = [(2 * q + c, 2 * (q ^ steps[i][c]) + c) for q in range(DIRECT) for c in range(2)]
+    return lax.ppermute(x, ("chip", "core"), pairs)
+
+
 def reduce_scatter(x):
     cores, chips = x.shape[:2]
-    if not (cores == 2 and chips > 1 and direct(chips)):
+    if not planar(cores, chips):
         return lax.psum_scatter(lax.psum_scatter(x, "core"), "chip")
     core, chip = lax.axis_index("core"), lax.axis_index("chip")
-    row = lambda c, r: lax.dynamic_slice(x, (c, chip ^ r) + (0,) * (x.ndim - 2), (1, 1) + x.shape[2:])[0, 0]
+
+    def row(c, i):
+        return lax.dynamic_slice(x, (c, chip ^ reach(SCATTER, c, i)) + (0,) * (x.ndim - 2), (1, 1) + x.shape[2:])[0, 0]
+
     up = lambda rows: permute(jnp.stack([row(1 - core, r) for r in rows]), "core", 1)
-    first = row(core, 1) + up([1])[0]
-    others = [r for r in range(chips) if r != 1]
-    theirs, _ = lax.optimization_barrier((up(others), first))
-    parts = [row(core, r) + theirs[i] for i, r in enumerate(others)]
-    parts.insert(1, first)
-    return tree([p if r == 0 else permute(p, "chip", r) for r, p in enumerate(parts)])
+    first = row(core, 0) + up([0])[0]
+    theirs, _ = lax.optimization_barrier((up(range(1, chips)), first))
+    parts = [first] + [row(core, i) + theirs[i - 1] for i in range(1, chips)]
+    return tree([swap(p, SCATTER, i) if i < chips - 1 else p for i, p in enumerate(parts)])
 
 
 def all_reduce(x, axis):
@@ -219,17 +235,17 @@
     return tree([x if r == 0 else permute(x, axis, r) for r in range(n)])
 
 
-def all_gather(own, outer, inner):
-    no, ni = lax.axis_size(outer), lax.axis_size(inner)
-    if not (direct(no) and direct(ni)):
-        return lax.all_gather(lax.all_gather(own, inner), outer)
-    mo, mi = lax.axis_index(outer), lax.axis_index(inner)
-    got = [own if r == 0 else permute(own, inner, r) for r in range(ni)]
-    out = jnp.zeros((no, ni) + own.shape, own.dtype)
-    for r, row in enumerate(got):
-        for q in range(no):
-            there = row if q == 0 else lax.ppermute(row, outer, partners(no, q))
-            out = lax.dynamic_update_slice(out, there[None, None], (mo ^ q, mi ^ r) + (0,) * own.ndim)
+def all_gather(own):
+    cores, chips = lax.axis_size("core"), lax.axis_size("chip")
+    if not planar(cores, chips):
+        return lax.all_gather(lax.all_gather(own, "chip"), "core")
+    core, chip = lax.axis_index("core"), lax.axis_index("chip")
+    got = [swap(own, SPREAD, i) for i in range(chips - 1)] + [own]
+    out = jnp.zeros((cores, chips) + own.shape, own.dtype)
+    for i in (3, 0, 1, 2):
+        there = lax.ppermute(got[i], "core", partners(2, 1))
+        for c, row in ((core, got[i]), (1 - core, there)):
+            out = lax.dynamic_update_slice(out, row[None, None], (c, chip ^ reach(SPREAD, c, i)) + (0,) * own.ndim)
     return out
 
 
@@ -244,7 +260,7 @@
     packed, modes, e_both, scales = head(snapshots, validation, e_rows, w_row, total, cores * chips * piece)
     own = reduce_scatter(packed.reshape(cores, chips, piece, LANES))
     own = all_reduce(own, "plane")
-    packed = all_gather(own, "core", "chip").reshape(-1, LANES)
+    packed = all_gather(own).reshape(-1, LANES)
     return tail(packed, modes, e_both, scales)
 
 

time: 36.9 us -> 34.5 us (0.935)
  waiting for transfers between devices: 18.2 us -> 15.7 us
    ppermute x11 -> x5, waiting for transfers between devices: 17 us -> 6.21 us  [permute(): return lax.ppermute(x, axis, partners(lax.axis_size(axis), r))]
    ppermute x4 -> x10, starting transfers between devices: 0.01 us -> 8.48 us  [the longest x6 8.36 us: swap(): return lax.ppermute(x, ('chip', 'core'), pairs)]
    ppermute x11 -> x5, starting transfers between devices: 13.5 us -> 5.09 us  [permute(): return lax.ppermute(x, axis, partners(lax.axis_size(axis), r))]
    ppermute x4 -> x10, waiting for transfers between devices: 1.19 us -> 9.47 us  [the longest x6 8.39 us: swap(): return lax.ppermute(x, ('chip', 'core'), pairs)]
  transfers between devices with their start and end apart: 15 -> 15, of which waited for: 10 -> 11; matrix products, arithmetic and copies ran while one was open for 0% -> 0% of each run, Pallas kernels for 0% -> 0%
where the time goes in v6:
time: 34.5 us; the launch traced here: 34.3 us
  waiting for transfers between devices  15.7 us (46%)
  starting transfers between devices  13.6 us (39%)
  Pallas kernels  4.04 us (12%)
  between operations  0.76 us (2%)
    ppermute x6, waiting for transfers between devices, swap(): return lax.ppermute(x, ('chip', 'core'), pairs)  8.39 us
    ppermute x6, starting transfers between devices, swap(): return lax.ppermute(x, ('chip', 'core'), pairs)  8.36 us
    ppermute x5, waiting for transfers between devices, permute(): return lax.ppermute(x, axis, partners(lax.axis_size(axis), r))  6.21 us
    ppermute x5, starting transfers between devices, permute(): return lax.ppermute(x, axis, partners(lax.axis_size(axis), r))  5.09 us
    pallas_call x1, Pallas kernels, head(): pl.pallas_call(functools.partial(head_kernel, total), out_shape=(pltpu.VM...  2.76 us
    pallas_call x1, Pallas kernels, tail(): pl.pallas_call(tail_kernel, out_shape=(pltpu.HBM((k, k), F32), pltpu.HBM(...  1.27 us
    ppermute x4, waiting for transfers between devices, all_gather(): there = lax.ppermute(got[i], 'core', partners(2, 1))  1.08 us
  transfers between devices with their start and end apart: 15, of which 11 were waited for; matrix products, arithmetic and copies ran while one was open for 0% of the time, Pallas kernels for 0%

profile of v6, /device:TPU:0, one launch (start us, length us, event | category | flops | bytes accessed | tf_op | source)
XLA Modules:
  0.0 34.3 jit_solution(3364348437964414781)
XLA Ops:
  0.7 2.8 %head.1 = (f32[1344,128]{1,0:T(8,128)S(1)}, f32[64,512]{1,0:T(8,128)S(1)}, bf16[128,512]{1,0:T(8,128)(2,1)S(1)}, f32[64,128]{1,0:T(8,128)S(1)}) custom-call(f32[512,512]{1,0:T(8,128)} %s_hbm.1, f32[512,512]{1,0:T(8,128)} %v_hbm.1, f32[64,512]{1,0:T(8,128)} %bitcast.53, f32[1,64]{1,0:T(1,128)} %bitcast.54), custom_call_target="tpu_custom_call" | custom-call | tf_op jit(solution)/shard_map/head/pallas_call | solution.py:111
  3.5 0.6 %collective-permute-start = (f32[1,168,128]{2,1,0:T(8,128)S(1)}, f32[1,168,128]{2,1,0:T(8,128)S(1)}, u32[]{:S(2)}, u32[]{:S(2)}) collective-permute-start(f32[1,168,128]{2,1,0:T(8,128)S(1)} %get-tuple-element.18), channel_id=1, source_target_pairs={{0,1},{1,0},{2,3},{3,2},{4,5},{5,4},{6,7},{7,6},{8,9},{9,8},{10,11... | collective-permute-start | bytes 258056 | tf_op jit(solution)/shard_map/ppermute | solution.py:199
  4.1 0.1 collective-permute-start.2
  4.1 0.8 %collective-permute-done = f32[1,168,128]{2,1,0:T(8,128)S(1)} collective-permute-done((f32[1,168,128]{2,1,0:T(8,128)S(1)}, f32[1,168,128]{2,1,0:T(8,128)S(1)}, u32[]{:S(2)}, u32[]{:S(2)}) %collective-permute-start) | collective-permute-done | bytes 86048 | tf_op jit(solution)/shard_map/ppermute | solution.py:199
  5.0 2.9 %collective-permute-start.1 = (f32[168,128]{1,0:T(8,128)S(1)}, f32[168,128]{1,0:T(8,128)S(1)}, u32[]{:S(2)}, u32[]{:S(2)}) collective-permute-start(f32[168,128]{1,0:T(8,128)S(1)} %bitcast_add_fusion.3), channel_id=1, source_target_pairs={{0,2},{1,3},{2,0},{3,1},{4,6},{5,7},{6,4},{7,5},{8,10},{9,11},{10,... | collective-permute-start | bytes 258056 | tf_op jit(solution)/shard_map/ppermute | solution.py:212
  7.9 0.0 collective-permute-done.2
  7.9 1.6 %collective-permute-start.3 = (f32[168,128]{1,0:T(8,128)S(1)}, f32[168,128]{1,0:T(8,128)S(1)}, u32[]{:S(2)}, u32[]{:S(2)}) collective-permute-start(f32[168,128]{1,0:T(8,128)S(1)} %get-tuple-element.16), channel_id=1, source_target_pairs={{0,4},{1,5},{2,6},{3,7},{4,0},{5,1},{6,2},{7,3},{8,12},{9,13},{10,... | collective-permute-start | bytes 258056 | tf_op jit(solution)/shard_map/ppermute | solution.py:212
  9.5 0.3 collective-permute-start.4
  9.8 0.9 %collective-permute-done.1 = f32[168,128]{1,0:T(8,128)S(1)} collective-permute-done((f32[168,128]{1,0:T(8,128)S(1)}, f32[168,128]{1,0:T(8,128)S(1)}, u32[]{:S(2)}, u32[]{:S(2)}) %collective-permute-start.1) | collective-permute-done | bytes 86048 | tf_op jit(solution)/shard_map/ppermute | solution.py:212
  10.7 2.6 %collective-permute-done.3 = f32[168,128]{1,0:T(8,128)S(1)} collective-permute-done((f32[168,128]{1,0:T(8,128)S(1)}, f32[168,128]{1,0:T(8,128)S(1)}, u32[]{:S(2)}, u32[]{:S(2)}) %collective-permute-start.3) | collective-permute-done | bytes 86048 | tf_op jit(solution)/shard_map/ppermute | solution.py:212
  13.4 1.5 %collective-permute-done.4 = f32[168,128]{1,0:T(8,128)S(1)} collective-permute-done((f32[168,128]{1,0:T(8,128)S(1)}, f32[168,128]{1,0:T(8,128)S(1)}, u32[]{:S(2)}, u32[]{:S(2)}) %collective-permute-start.4) | collective-permute-done | bytes 86048 | tf_op jit(solution)/shard_map/ppermute | solution.py:212
  14.9 3.7 %collective-permute-start.7 = (f32[168,128]{1,0:T(8,128)S(1)}, f32[168,128]{1,0:T(8,128)S(1)}, u32[]{:S(2)}, u32[]{:S(2)}) collective-permute-start(f32[168,128]{1,0:T(8,128)S(1)} %fusion.1), channel_id=1, source_target_pairs={{0,24},{8,16},{16,8},{24,0},{1,25},{9,17},{17,9},{25,1},{2,26},{10... | collective-permute-start | bytes 258056 | tf_op jit(solution)/shard_map/ppermute | solution.py:199
  18.6 0.0 collective-permute-start.6
  18.6 0.8 %collective-permute-start.5 = (f32[168,128]{1,0:T(8,128)S(1)}, f32[168,128]{1,0:T(8,128)S(1)}, u32[]{:S(2)}, u32[]{:S(2)}) collective-permute-start(f32[168,128]{1,0:T(8,128)S(1)} %fusion.1), channel_id=1, source_target_pairs={{0,8},{8,0},{16,24},{24,16},{1,9},{9,1},{17,25},{25,17},{2,10},{10... | collective-permute-start | bytes 258056 | tf_op jit(solution)/shard_map/ppermute | solution.py:199
  19.4 1.9 %collective-permute-done.7 = f32[168,128]{1,0:T(8,128)S(1)} collective-permute-done((f32[168,128]{1,0:T(8,128)S(1)}, f32[168,128]{1,0:T(8,128)S(1)}, u32[]{:S(2)}, u32[]{:S(2)}) %collective-permute-start.7) | collective-permute-done | bytes 86048 | tf_op jit(solution)/shard_map/ppermute | solution.py:199
  21.3 3.5 %collective-permute-done.6 = f32[168,128]{1,0:T(8,128)S(1)} collective-permute-done((f32[168,128]{1,0:T(8,128)S(1)}, f32[168,128]{1,0:T(8,128)S(1)}, u32[]{:S(2)}, u32[]{:S(2)}) %collective-permute-start.6) | collective-permute-done | bytes 86048 | tf_op jit(solution)/shard_map/ppermute | solution.py:199
  24.7 0.0 collective-permute-done.5
  24.8 0.7 %collective-permute-start.11 = (f32[168,128]{1,0:T(8,128)S(1)}, f32[168,128]{1,0:T(8,128)S(1)}, u32[]{:S(2)}, u32[]{:S(2)}) collective-permute-start(f32[168,128]{1,0:T(8,128)S(1)} %get-tuple-element.15), channel_id=1, source_target_pairs={{0,4},{1,3},{2,6},{3,1},{4,0},{5,7},{6,2},{7,5},{8,12},{9,11},{10,... | collective-permute-start | bytes 258056 | tf_op jit(solution)/shard_map/ppermute | solution.py:212
  25.5 1.7 %collective-permute-start.9 = (f32[168,128]{1,0:T(8,128)S(1)}, f32[168,128]{1,0:T(8,128)S(1)}, u32[]{:S(2)}, u32[]{:S(2)}) collective-permute-start(f32[168,128]{1,0:T(8,128)S(1)} %get-tuple-element.15), channel_id=1, source_target_pairs={{0,6},{1,7},{2,4},{3,5},{4,2},{5,3},{6,0},{7,1},{8,14},{9,15},{10,... | collective-permute-start | bytes 258056 | tf_op jit(solution)/shard_map/ppermute | solution.py:212
  27.2 0.0 collective-permute-start.8
  27.2 1.2 %collective-permute-start.13 = (f32[168,128]{1,0:T(8,128)S(1)}, f32[168,128]{1,0:T(8,128)S(1)}, u32[]{:S(2)}, u32[]{:S(2)}) collective-permute-start(f32[168,128]{1,0:T(8,128)S(1)} %get-tuple-element.15), channel_id=1, source_target_pairs={{0,2},{1,5},{2,0},{3,7},{4,6},{5,1},{6,4},{7,3},{8,10},{9,13},{10,... | collective-permute-start | bytes 258056 | tf_op jit(solution)/shard_map/ppermute | solution.py:212
  28.4 1.7 %collective-permute-done.11 = f32[168,128]{1,0:T(8,128)S(1)} collective-permute-done((f32[168,128]{1,0:T(8,128)S(1)}, f32[168,128]{1,0:T(8,128)S(1)}, u32[]{:S(2)}, u32[]{:S(2)}) %collective-permute-start.11) | collective-permute-done | bytes 86048 | tf_op jit(solution)/shard_map/ppermute | solution.py:212
  30.0 0.0 collective-permute-start.12
  30.0 0.9 %collective-permute-done.9 = f32[168,128]{1,0:T(8,128)S(1)} collective-permute-done((f32[168,128]{1,0:T(8,128)S(1)}, f32[168,128]{1,0:T(8,128)S(1)}, u32[]{:S(2)}, u32[]{:S(2)}) %collective-permute-start.9) | collective-permute-done | bytes 86048 | tf_op jit(solution)/shard_map/ppermute | solution.py:212
  31.0 0.0 collective-permute-start.10
  31.0 0.0 collective-permute-done.8
  31.0 0.7 %collective-permute-done.13 = f32[168,128]{1,0:T(8,128)S(1)} collective-permute-done((f32[168,128]{1,0:T(8,128)S(1)}, f32[168,128]{1,0:T(8,128)S(1)}, u32[]{:S(2)}, u32[]{:S(2)}) %collective-permute-start.13) | collective-permute-done | bytes 86048 | tf_op jit(solution)/shard_map/ppermute | solution.py:212
  31.8 0.1 collective-permute-start.14
  31.9 0.4 %collective-permute-done.10 = f32[168,128]{1,0:T(8,128)S(1)} collective-permute-done((f32[168,128]{1,0:T(8,128)S(1)}, f32[168,128]{1,0:T(8,128)S(1)}, u32[]{:S(2)}, u32[]{:S(2)}) %collective-permute-start.10) | collective-permute-done | bytes 86048 | tf_op jit(solution)/shard_map/ppermute | solution.py:246
  32.3 0.0 collective-permute-done.12
  32.4 0.7 %collective-permute-done.14 = f32[168,128]{1,0:T(8,128)S(1)} collective-permute-done((f32[168,128]{1,0:T(8,128)S(1)}, f32[168,128]{1,0:T(8,128)S(1)}, u32[]{:S(2)}, u32[]{:S(2)}) %collective-permute-start.14) | collective-permute-done | bytes 86048 | tf_op jit(solution)/shard_map/ppermute | solution.py:246
  33.1 1.3 %tail.1 = (f32[512,512]{1,0:T(8,128)}, f32[64,512]{1,0:T(8,128)}, f32[64,512]{1,0:T(8,128)}, f32[64,512]{1,0:T(8,128)}) custom-call(f32[1344,128]{1,0:T(8,128)S(1)} %bitcast.48, f32[64,512]{1,0:T(8,128)S(1)} %get-tuple-element.11.modes_ref, bf16[128,512]{1,0:T(8,128)(2,1)S(1)} %get-tuple-element.12.e_ref, f32[64,128]{1,0:T(8,128)S(1)} %get-tuple-element.13.scale_ref), custom_call_target="tpu_custom_call" | custom-call | tf_op jit(solution)/shard_map/tail/pallas_call | solution.py:173
  (14 shorter events, 0.3 us)
Async XLA Ops:
  3.5 1.5 %collective-permute-start = (f32[1,168,128]{2,1,0:T(8,128)S(1)}, f32[1,168,128]{2,1,0:T(8,128)S(1)}, u32[]{:S(2)}, u32[]{:S(2)}) collective-permute-start(f32[1,168,128]{2,1,0:T(8,128)S(1)} %get-tuple-element.18), channel_id=1, source_target_pairs={{0,1},{1,0},{2,3},{3,2},{4,5},{5,4},{6,7},{7,6},{8,9},{9,8},{10,11... | collective-permute-start | bytes 258056 | tf_op jit(solution)/shard_map/ppermute | solution.py:199
  4.1 3.8 %collective-permute-start.2 = (f32[3,168,128]{2,1,0:T(8,128)S(1)}, f32[3,168,128]{2,1,0:T(8,128)S(1)}, u32[]{:S(2)}, u32[]{:S(2)}) collective-permute-start(f32[3,168,128]{2,1,0:T(8,128)S(1)} %pad_maximum_fusion), channel_id=1, source_target_pairs={{0,1},{1,0},{2,3},{3,2},{4,5},{5,4},{6,7},{7,6},{8,9},{9,8},{10,11... | collective-permute-start | bytes 774152 | tf_op jit(solution)/shard_map/ppermute | solution.py:199
  5.0 5.7 %collective-permute-start.1 = (f32[168,128]{1,0:T(8,128)S(1)}, f32[168,128]{1,0:T(8,128)S(1)}, u32[]{:S(2)}, u32[]{:S(2)}) collective-permute-start(f32[168,128]{1,0:T(8,128)S(1)} %bitcast_add_fusion.3), channel_id=1, source_target_pairs={{0,2},{1,3},{2,0},{3,1},{4,6},{5,7},{6,4},{7,5},{8,10},{9,11},{10,... | collective-permute-start | bytes 258056 | tf_op jit(solution)/shard_map/ppermute | solution.py:212
  7.9 5.5 %collective-permute-start.3 = (f32[168,128]{1,0:T(8,128)S(1)}, f32[168,128]{1,0:T(8,128)S(1)}, u32[]{:S(2)}, u32[]{:S(2)}) collective-permute-start(f32[168,128]{1,0:T(8,128)S(1)} %get-tuple-element.16), channel_id=1, source_target_pairs={{0,4},{1,5},{2,6},{3,7},{4,0},{5,1},{6,2},{7,3},{8,12},{9,13},{10,... | collective-permute-start | bytes 258056 | tf_op jit(solution)/shard_map/ppermute | solution.py:212
  9.5 5.4 %collective-permute-start.4 = (f32[168,128]{1,0:T(8,128)S(1)}, f32[168,128]{1,0:T(8,128)S(1)}, u32[]{:S(2)}, u32[]{:S(2)}) collective-permute-start(f32[168,128]{1,0:T(8,128)S(1)} %get-tuple-element.17), channel_id=1, source_target_pairs={{0,6},{1,7},{2,4},{3,5},{4,2},{5,3},{6,0},{7,1},{8,14},{9,15},{10,... | collective-permute-start | bytes 258056 | tf_op jit(solution)/shard_map/ppermute | solution.py:212
  14.9 6.4 %collective-permute-start.7 = (f32[168,128]{1,0:T(8,128)S(1)}, f32[168,128]{1,0:T(8,128)S(1)}, u32[]{:S(2)}, u32[]{:S(2)}) collective-permute-start(f32[168,128]{1,0:T(8,128)S(1)} %fusion.1), channel_id=1, source_target_pairs={{0,24},{8,16},{16,8},{24,0},{1,25},{9,17},{17,9},{25,1},{2,26},{10... | collective-permute-start | bytes 258056 | tf_op jit(solution)/shard_map/ppermute | solution.py:199
  18.6 6.2 %collective-permute-start.6 = (f32[168,128]{1,0:T(8,128)S(1)}, f32[168,128]{1,0:T(8,128)S(1)}, u32[]{:S(2)}, u32[]{:S(2)}) collective-permute-start(f32[168,128]{1,0:T(8,128)S(1)} %fusion.1), channel_id=1, source_target_pairs={{0,16},{8,24},{16,0},{24,8},{1,17},{9,25},{17,1},{25,9},{2,18},{10... | collective-permute-start | bytes 258056 | tf_op jit(solution)/shard_map/ppermute | solution.py:199
  18.6 6.2 %collective-permute-start.5 = (f32[168,128]{1,0:T(8,128)S(1)}, f32[168,128]{1,0:T(8,128)S(1)}, u32[]{:S(2)}, u32[]{:S(2)}) collective-permute-start(f32[168,128]{1,0:T(8,128)S(1)} %fusion.1), channel_id=1, source_target_pairs={{0,8},{8,0},{16,24},{24,16},{1,9},{9,1},{17,25},{25,17},{2,10},{10... | collective-permute-start | bytes 258056 | tf_op jit(solution)/shard_map/ppermute | solution.py:199
  24.8 5.2 %collective-permute-start.11 = (f32[168,128]{1,0:T(8,128)S(1)}, f32[168,128]{1,0:T(8,128)S(1)}, u32[]{:S(2)}, u32[]{:S(2)}) collective-permute-start(f32[168,128]{1,0:T(8,128)S(1)} %get-tuple-element.15), channel_id=1, source_target_pairs={{0,4},{1,3},{2,6},{3,1},{4,0},{5,7},{6,2},{7,5},{8,12},{9,11},{10,... | collective-permute-start | bytes 258056 | tf_op jit(solution)/shard_map/ppermute | solution.py:212
  25.5 5.5 %collective-permute-start.9 = (f32[168,128]{1,0:T(8,128)S(1)}, f32[168,128]{1,0:T(8,128)S(1)}, u32[]{:S(2)}, u32[]{:S(2)}) collective-permute-start(f32[168,128]{1,0:T(8,128)S(1)} %get-tuple-element.15), channel_id=1, source_target_pairs={{0,6},{1,7},{2,4},{3,5},{4,2},{5,3},{6,0},{7,1},{8,14},{9,15},{10,... | collective-permute-start | bytes 258056 | tf_op jit(solution)/shard_map/ppermute | solution.py:212
  27.2 3.8 %collective-permute-start.8 = (f32[168,128]{1,0:T(8,128)S(1)}, f32[168,128]{1,0:T(8,128)S(1)}, u32[]{:S(2)}, u32[]{:S(2)}) collective-permute-start(f32[168,128]{1,0:T(8,128)S(1)} %get-tuple-element.15), channel_id=1, source_target_pairs={{0,1},{1,0},{2,3},{3,2},{4,5},{5,4},{6,7},{7,6},{8,9},{9,8},{10,11... | collective-permute-start | bytes 258056 | tf_op jit(solution)/shard_map/ppermute | solution.py:246
  27.2 4.5 %collective-permute-start.13 = (f32[168,128]{1,0:T(8,128)S(1)}, f32[168,128]{1,0:T(8,128)S(1)}, u32[]{:S(2)}, u32[]{:S(2)}) collective-permute-start(f32[168,128]{1,0:T(8,128)S(1)} %get-tuple-element.15), channel_id=1, source_target_pairs={{0,2},{1,5},{2,0},{3,7},{4,6},{5,1},{6,4},{7,3},{8,10},{9,13},{10,... | collective-permute-start | bytes 258056 | tf_op jit(solution)/shard_map/ppermute | solution.py:212
  30.0 2.3 %collective-permute-start.12 = (f32[168,128]{1,0:T(8,128)S(1)}, f32[168,128]{1,0:T(8,128)S(1)}, u32[]{:S(2)}, u32[]{:S(2)}) collective-permute-start(f32[168,128]{1,0:T(8,128)S(1)} %collective-permute-done.11), channel_id=1, source_target_pairs={{0,1},{1,0},{2,3},{3,2},{4,5},{5,4},{6,7},{7,6},{8,9},{9,8},{10,11... | collective-permute-start | bytes 258056 | tf_op jit(solution)/shard_map/ppermute | solution.py:246
  31.0 1.3 %collective-permute-start.10 = (f32[168,128]{1,0:T(8,128)S(1)}, f32[168,128]{1,0:T(8,128)S(1)}, u32[]{:S(2)}, u32[]{:S(2)}) collective-permute-start(f32[168,128]{1,0:T(8,128)S(1)} %collective-permute-done.9), channel_id=1, source_target_pairs={{0,1},{1,0},{2,3},{3,2},{4,5},{5,4},{6,7},{7,6},{8,9},{9,8},{10,11... | collective-permute-start | bytes 258056 | tf_op jit(solution)/shard_map/ppermute | solution.py:246
  31.8 1.3 %collective-permute-start.14 = (f32[168,128]{1,0:T(8,128)S(1)}, f32[168,128]{1,0:T(8,128)S(1)}, u32[]{:S(2)}, u32[]{:S(2)}) collective-permute-start(f32[168,128]{1,0:T(8,128)S(1)} %collective-permute-done.13), channel_id=1, source_target_pairs={{0,1},{1,0},{2,3},{3,2},{4,5},{5,4},{6,7},{7,6},{8,9},{9,8},{10,11... | collective-permute-start | bytes 258056 | tf_op jit(solution)/shard_map/ppermute | solution.py:246
